TPU v7x, 128 devices: a whole 4x4x4 slice. The times are simulated.
128 devices in a mesh: rep: 2 (over core), dp: 64 (over x, y, z).
Axes of the slice: x: 4, y: 4, z: 4, core: 2. Of those that a mesh axis runs over, the one named last changes fastest.
Arguments:
- x: bfloat16 [128, 2048, 896], P(('rep', 'dp')), parts along dimension 0
- dy: bfloat16 [128, 2048, 896], P(('rep', 'dp')), parts along dimension 0
- w_gate: bfloat16 [2, 896, 2560], P(None, 'dp')
- w_up: bfloat16 [2, 896, 2560], P(None, 'dp')
- w_down: bfloat16 [2, 2560, 896], P(None, 'dp')
Outputs:
- output 1: bfloat16 [128, 2048, 896], P(('rep', 'dp')), parts along dimension 0
- output 2: bfloat16 [4, 896, 2560], P('rep', 'dp'), parts along dimension 0
- output 3: bfloat16 [4, 896, 2560], P('rep', 'dp'), parts along dimension 0
- output 4: bfloat16 [4, 2560, 896], P('rep', 'dp'), parts along dimension 0
There are 2 independent parts. A program takes and returns all parts, laid end to end along the dimension named above; an argument that names none is the same for every part.
All inputs are finite; a program needn't handle non-finite values.
Results may differ from a plain program's by a relative error of at most 0.018.
Values are sent between devices in bfloat16 or wider.
A program may use at most 1.5 GiB of HBM per device.

v0:
```python
import jax
import jax.numpy as jnp
from jax import lax

NAMES = ("w_gate", "w_up", "w_down")


def matmul(a, w):
    return jnp.dot(a, w, preferred_element_type=jnp.float32).astype(jnp.bfloat16)


def normed(h):
    wide = h.astype(jnp.float32)
    scale = lax.rsqrt(jnp.mean(wide**2, -1, keepdims=True) + 1e-6)
    return (wide * scale).astype(jnp.bfloat16)


def layer(h, w):
    a = normed(h)
    gate = jnp.dot(a, w["w_gate"], preferred_element_type=jnp.float32)
    up = jnp.dot(a, w["w_up"], preferred_element_type=jnp.float32)
    return h + matmul((jax.nn.silu(gate) * up).astype(jnp.bfloat16), w["w_down"])


def stack(weights, h):
    for number in range(weights["w_gate"].shape[0]):
        h = layer(h, {name: w[number] for name, w in weights.items()})
    return h


def solution(mesh):
    groups = mesh.shape["rep"]

    def step(x, dy, *weights):
        shape = x.shape
        x, dy = (t.reshape(groups, -1, *t.shape[1:]) for t in (x, dy))

        def of_a_group(x, dy):
            _, back = jax.vjp(stack, dict(zip(NAMES, weights, strict=True)), x)
            by_weights, by_x = back(dy)
            return (by_x, *(by_weights[name] for name in NAMES))

        by_x, *by_weights = jax.vmap(of_a_group)(x, dy)
        return (by_x.reshape(shape), *(t.reshape(-1, *t.shape[2:]) for t in by_weights))

    return step
```

profile of v0, /device:TPU:0, one launch (start us, length us, event | category | flops | bytes accessed | tf_op | source)
XLA Modules:
  0.0 1557.4 jit_solution(6002440863662340368)
XLA Ops:
  14.6 2.8 fusion.36
  17.5 6.1 copy.15
  24.1 6.2 copy.14
  30.3 63.6 %all-gather.29.cloned.1.call-done = bf16[1,896,2560]{2,0,1:T(2,128)(2,1)} async-done(((bf16[1,14,2560]{2,0,1:T(2,128)(2,1)}), bf16[1,896,2560]{2,0,1:T(2,128)(2,1)}) %all-gather.29.cloned.1.call-update) | async-done | bytes 4587536 | tf_op jit(solution)/vmap(jvp())/squeeze | solution.py:27
  94.0 18.8 %fusion.68 = f32[2048,2560]{1,0:T(8,128)} fusion(bf16[1,896,2560]{2,0,1:T(2,128)(2,1)} %all-gather.29.cloned.1.call-done, bf16[1,2048,896]{2,1,0:T(8,128)(2,1)} %param.1, f32[2048]{0:T(1024)S(1)} %get-tuple-element.57), kind=kOutput, calls=%fused_computation.83 | convolution fusion | flops 9400745984 | bytes 29237248 | tf_op jit(solution)/vmap(jvp())/dot_general | solution.py:20
  112.8 64.8 %all-gather.31.cloned.1.call-done = bf16[1,896,2560]{2,0,1:T(2,128)(2,1)} async-done(((bf16[1,14,2560]{2,0,1:T(2,128)(2,1)}), bf16[1,896,2560]{2,0,1:T(2,128)(2,1)}) %all-gather.31.cloned.1.call-update) | async-done | bytes 4587536 | tf_op jit(solution)/vmap(jvp())/squeeze | solution.py:27
  177.6 19.0 %fusion.64 = f32[2048,2560]{1,0:T(8,128)} fusion(bf16[1,896,2560]{2,0,1:T(2,128)(2,1)} %all-gather.31.cloned.1.call-done, bf16[1,2048,896]{2,1,0:T(8,128)(2,1)} %param.1, f32[2048]{0:T(1024)S(1)} %get-tuple-element.57), kind=kOutput, calls=%fused_computation.79 | convolution fusion | flops 9400745984 | bytes 29237248 | tf_op jit(solution)/vmap(jvp())/dot_general | solution.py:21
  196.6 19.6 %fusion.28 = bf16[2048,2560]{1,0:T(8,128)(2,1)} fusion(f32[2048,2560]{1,0:T(8,128)} %fusion.64, f32[2048,2560]{1,0:T(8,128)} %fusion.68), kind=kLoop, calls=%fused_computation.43 | loop fusion | flops 31457280 | bytes 52428800
  216.2 32.4 %all-gather.33.cloned.1.call-done = bf16[1,2560,896]{2,1,0:T(8,128)(2,1)} async-done(((bf16[1,40,896]{2,1,0:T(8,128)(2,1)}), bf16[1,2560,896]{2,1,0:T(8,128)(2,1)}) %all-gather.33.cloned.1.call-update) | async-done | bytes 4587536 | tf_op jit(solution)/vmap(jvp())/squeeze | solution.py:27
  248.6 16.2 %fusion.44 = (f32[2048]{0:T(1024)S(1)}, bf16[1,1,2048,896]{2,3,1,0:T(8,128)(2,1)}) fusion(bf16[2048,2560]{1,0:T(8,128)(2,1)} %fusion.28, bf16[1,2560,896]{2,1,0:T(8,128)(2,1)} %all-gather.33.cloned.1.call-done, bf16[1,2048,896]{1,2,0:T(8,128)(2,1)} %copy.15), kind=kOutput, calls=%fused_computation.62 | convolution fusion | flops 9404413952 | bytes 22421504 | tf_op jit(solution)/vmap(jvp())/dot_general | solution.py:9
  265.4 65.0 %all-gather.35.cloned.1.call-done = bf16[1,896,2560]{2,0,1:T(2,128)(2,1)} async-done(((bf16[1,14,2560]{2,0,1:T(2,128)(2,1)}), bf16[1,896,2560]{2,0,1:T(2,128)(2,1)}) %all-gather.35.cloned.1.call-update) | async-done | bytes 4587536 | tf_op jit(solution)/vmap(jvp())/squeeze | solution.py:27
  330.4 19.3 %fusion.61 = f32[2048,2560]{1,0:T(8,128)} fusion(bf16[1,1,2048,896]{2,3,1,0:T(8,128)(2,1)} %get-tuple-element.59, f32[2048]{0:T(1024)S(1)} %bitcast.329, bf16[1,896,2560]{2,0,1:T(2,128)(2,1)} %all-gather.35.cloned.1.call-done), kind=kOutput, calls=%fused_computation.76 | convolution fusion | flops 9400745984 | bytes 29237248 | tf_op jit(solution)/vmap(jvp())/dot_general | solution.py:20
  349.8 64.1 %all-gather.39.cloned.1.call-done = bf16[1,896,2560]{2,0,1:T(2,128)(2,1)} async-done(((bf16[1,14,2560]{2,0,1:T(2,128)(2,1)}), bf16[1,896,2560]{2,0,1:T(2,128)(2,1)}) %all-gather.39.cloned.1.call-update) | async-done | bytes 4587536 | tf_op jit(solution)/vmap(jvp())/squeeze | solution.py:27
  413.9 19.0 %fusion.56 = f32[2048,2560]{1,0:T(8,128)} fusion(bf16[1,1,2048,896]{2,3,1,0:T(8,128)(2,1)} %get-tuple-element.59, f32[2048]{0:T(1024)S(1)} %bitcast.330, bf16[1,896,2560]{2,0,1:T(2,128)(2,1)} %all-gather.39.cloned.1.call-done), kind=kOutput, calls=%fused_computation.71 | convolution fusion | flops 9400745984 | bytes 29237248 | tf_op jit(solution)/vmap(jvp())/dot_general | solution.py:21
  432.9 51.8 %all-gather.37.cloned.1.call-done = bf16[1,2560,896]{2,1,0:T(8,128)(2,1)} async-done(((bf16[1,40,896]{2,1,0:T(8,128)(2,1)}), bf16[1,2560,896]{2,1,0:T(8,128)(2,1)}) %all-gather.37.cloned.1.call-update) | async-done | bytes 4587536 | tf_op jit(solution)/vmap(jvp())/squeeze | solution.py:27
  484.7 14.2 convolution_convert_fusion.1
  498.9 24.3 %fusion.8 = bf16[2048,2560]{1,0:T(8,128)(2,1)} fusion(f32[2048,2560]{1,0:T(8,128)} %fusion.61, f32[2048,2560]{1,0:T(8,128)} %fusion.56, bf16[2048,2560]{1,0:T(8,128)(2,1)S(1)} %convolution_convert_fusion.1), kind=kLoop, calls=%fused_computation.10 | loop fusion | flops 62914560 | bytes 62914560
  523.2 16.5 %fusion.59 = bf16[2048,896]{0,1:T(8,128)(2,1)} fusion(bf16[2048,2560]{1,0:T(8,128)(2,1)} %fusion.8, bf16[1,896,2560]{2,0,1:T(2,128)(2,1)} %all-gather.35.cloned.1.call-done), kind=kOutput, calls=%fused_computation.74 | convolution fusion | flops 9395240960 | bytes 18743296 | tf_op jit(solution)/vmap(transpose(jvp()))/dot_general | solution.py:20
  539.7 20.1 %fusion.46 = (f32[2048]{0:T(1024)S(1)}, bf16[2048,896]{0,1:T(8,128)(2,1)S(1)}) fusion(bf16[1,1,2048,896]{2,3,1,0:T(8,128)(2,1)S(1)} %copy-done.5, bf16[2048,896]{0,1:T(8,128)(2,1)} %fusion.59, bf16[1,896,2560]{2,0,1:T(2,128)(2,1)} %all-gather.39.cloned.1.call-done, bf16[2048,2560]{1,0:T(8,128)(2,1)} %copy-done.3, f32[2048,2560]{1,0:T(8,128)} %fusion.61), kind=kOutput, calls=%fused_computation.64 | convolution fusion | flops 9437706240 | bytes 47063040 | tf_op jit(solution)/vmap(transpose(jvp()))/dot_general | solution.py:21
  564.4 16.1 %convolution_bitcast_fusion = f32[1,2560,896]{2,1,0:T(8,128)} fusion(bf16[2048,2560]{1,0:T(8,128)(2,1)} %fusion.28, bf16[1,1,2048,896]{2,3,1,0:T(8,128)(2,1)S(1)} %fusion.78), kind=kOutput, calls=%fused_computation.68 | convolution fusion | flops 9395240960 | bytes 23330816 | tf_op jit(solution)/vmap(transpose(jvp()))/dot_general | solution.py:9
  580.6 14.6 convolution_convert_fusion
  595.2 3.8 copy-done.4
  599.0 21.4 %fusion.11 = bf16[2048,2560]{1,0:T(8,128)(2,1)} fusion(f32[2048,2560]{1,0:T(8,128)} %fusion.68, f32[2048,2560]{1,0:T(8,128)} %fusion.64, bf16[2048,2560]{1,0:T(8,128)(2,1)S(1)} %convolution_convert_fusion), kind=kLoop, calls=%fused_computation.13 | loop fusion | flops 62914560 | bytes 62914560
  620.4 16.5 %fusion.66 = bf16[2048,896]{0,1:T(8,128)(2,1)} fusion(bf16[2048,2560]{1,0:T(8,128)(2,1)} %fusion.11, bf16[1,896,2560]{2,0,1:T(2,128)(2,1)} %all-gather.29.cloned.1.call-done), kind=kOutput, calls=%fused_computation.81 | convolution fusion | flops 9395240960 | bytes 18743296 | tf_op jit(solution)/vmap(transpose(jvp()))/dot_general | solution.py:20
  636.9 17.1 %fusion.42 = (f32[2048]{0:T(1024)S(1)}, bf16[2048,896]{0,1:T(8,128)(2,1)}) fusion(bf16[1,2048,896]{1,2,0:T(8,128)(2,1)S(1)} %copy-done, bf16[2048,896]{0,1:T(8,128)(2,1)} %fusion.66, bf16[1,896,2560]{2,0,1:T(2,128)(2,1)S(1)} %bitcast.342, bf16[2048,2560]{1,0:T(8,128)(2,1)} %copy-done.4, f32[2048,2560]{1,0:T(8,128)} %fusion.68), kind=kOutput, calls=%fused_computation.60 | convolution fusion | flops 9437706240 | bytes 47063040 | tf_op jit(solution)/vmap(transpose(jvp()))/dot_general | solution.py:21
  654.6 14.5 convolution_bitcast_fusion.1
  669.1 22.0 %fusion.47 = f32[1,2560,896]{2,1,0:T(8,128)} fusion(f32[2048,2560]{1,0:T(8,128)} %fusion.56, f32[2048,2560]{1,0:T(8,128)} %fusion.61, bf16[1,2048,896]{2,1,0:T(8,128)(2,1)} %param), kind=kOutput, calls=%fused_computation.65 | convolution fusion | flops 9426698240 | bytes 54788096 | tf_op jit(solution)/vmap(transpose(jvp()))/dot_general | solution.py:9
  691.1 19.7 %fusion.53 = f32[1,896,2560]{2,1,0:T(8,128)} fusion(bf16[2048,2560]{1,0:T(8,128)(2,1)} %copy-done.4, f32[2048,2560]{1,0:T(8,128)} %fusion.68, bf16[1,2048,896]{1,2,0:T(8,128)(2,1)} %copy.15, f32[2048]{0:T(1024)S(1)} %bitcast.335), kind=kOutput, calls=%fused_computation.67 | convolution fusion | flops 9432203264 | bytes 44310528 | tf_op jit(solution)/vmap(transpose(jvp()))/dot_general | solution.py:21
  711.4 15.5 convolution_bitcast_fusion.2
  727.0 19.5 %fusion.50 = f32[1,896,2560]{2,1,0:T(8,128)} fusion(bf16[2048,2560]{1,0:T(8,128)(2,1)} %copy-done.3, f32[2048,2560]{1,0:T(8,128)} %fusion.61, bf16[1,1,2048,896]{2,3,1,0:T(8,128)(2,1)} %get-tuple-element.59, f32[2048]{0:T(1024)S(1)} %bitcast.333), kind=kOutput, calls=%fused_computation.66 | convolution fusion | flops 9432203264 | bytes 44310528 | tf_op jit(solution)/vmap(transpose(jvp()))/dot_general | solution.py:21
  746.5 667.2 %fusion.120 = (f32[16,2560]{1,0:T(8,128)S(1)}, f32[16,2560]{1,0:T(8,128)S(1)}, f32[16,2560]{1,0:T(8,128)S(1)}, f32[16,2560]{1,0:T(8,128)S(1)}) fusion(f32[1,896,2560]{2,1,0:T(8,128)} %convolution_bitcast_fusion.1, f32[1,896,2560]{2,1,0:T(8,128)} %convolution_bitcast_fusion.2, f32[1,896,2560]{2,1,0:T(8,128)} %fusion.53, f32[1,896,2560]{2,1,0:T(8,128)} %fusion.50), kind=kCustom, calls=%all-reduce-scatter.4 | all-reduce-scatter fusion | flops 10485761 | bytes 37356032
  1420.3 3.0 collective-permute-start.19
  1423.4 7.8 collective-permute-start.7
  1434.8 6.7 collective-permute-start.21
  1441.5 6.1 collective-permute-start.22
  1449.1 3.4 collective-permute-start.25
  1453.7 7.6 collective-permute-start.26
  1462.7 4.5 collective-permute-start.28
  1467.2 6.6 collective-permute-start.29
  1473.8 5.2 collective-permute-start.30
  1479.1 9.1 fusion.77
  1488.2 6.1 copy.16
  1498.3 3.4 collective-permute-start.1
  1501.7 4.2 collective-permute-start.2
  1513.1 6.7 collective-permute-start.5
  1519.8 5.5 collective-permute-start.6
  1527.0 2.8 collective-permute-start.11
  1538.5 4.0 collective-permute-start.9
  (132 shorter events, 57.1 us)
Async XLA Ops:
  7.2 86.8 %all-gather.29.cloned.1.call-start = ((), (), s32[]{:S(2)}) async-start(), calls=%async_computation.2 | async-start | bytes 9318400 | tf_op jit(solution)/vmap(jvp())/squeeze | solution.py:27
  9.2 168.4 %all-gather.31.cloned.1.call-start = ((), (), s32[]{:S(2)}) async-start(), calls=%async_computation.3 | async-start | bytes 9318400 | tf_op jit(solution)/vmap(jvp())/squeeze | solution.py:27
  11.2 237.4 %all-gather.33.cloned.1.call-start = ((), (), s32[]{:S(2)}) async-start(), calls=%async_computation.4 | async-start | bytes 4659200 | tf_op jit(solution)/vmap(jvp())/squeeze | solution.py:27
  12.9 317.6 %all-gather.35.cloned.1.call-start = ((), (), s32[]{:S(2)}) async-start(), calls=%async_computation.5 | async-start | bytes 9318400 | tf_op jit(solution)/vmap(jvp())/squeeze | solution.py:27
  13.4 400.4 %all-gather.39.cloned.1.call-start = ((), (), s32[]{:S(2)}) async-start(), calls=%async_computation.7 | async-start | bytes 9318400 | tf_op jit(solution)/vmap(jvp())/squeeze | solution.py:27
  14.0 470.7 %all-gather.37.cloned.1.call-start = ((), (), s32[]{:S(2)}) async-start(), calls=%async_computation.6 | async-start | bytes 4659200 | tf_op jit(solution)/vmap(jvp())/squeeze | solution.py:27
  14.6 1532.9 %reduce-scatter.31.cloned.1.call-start = ((), (), s32[]{:S(2)}) async-start(), calls=%async_computation.9 | async-start | bytes 9318400
  265.4 294.4 %copy-start.8 = (f32[1,1,2048]{2,1,0:T(1,128)}, f32[1,1,2048]{2,1,0:T(1,128)S(1)}, u32[]{:S(2)}) copy-start(f32[1,1,2048]{2,1,0:T(1,128)S(1)} %rsqrt.23) | copy-start | bytes 24580
  498.9 24.3 %copy-start.3 = (bf16[2048,2560]{1,0:T(8,128)(2,1)}, bf16[2048,2560]{1,0:T(8,128)(2,1)S(1)}, u32[]{:S(2)}) copy-start(bf16[2048,2560]{1,0:T(8,128)(2,1)S(1)} %convolution_convert_fusion.1) | copy-start | bytes 31457284
  539.7 20.1 %copy-start.7 = (f32[2048]{0:T(1024)S(1)}, f32[2048]{0:T(1024)}, u32[]{:S(2)}) copy-start(f32[2048]{0:T(1024)} %copy-done.6) | copy-start | bytes 24580
  539.7 20.1 %copy-start.1 = (bf16[1,2048,896]{1,2,0:T(8,128)(2,1)S(1)}, bf16[1,2048,896]{1,2,0:T(8,128)(2,1)}, u32[]{:S(2)}) copy-start(bf16[1,2048,896]{1,2,0:T(8,128)(2,1)} %copy.14) | copy-start | bytes 11010052
  580.5 967.9 %reduce-scatter.29.cloned.1.call-start = ((), (), s32[]{:S(2)}) async-start(), calls=%async_computation.8 | async-start | bytes 9318400
  599.0 37.8 %slice-start = ((s8[9175040]{0:T(1024)(128)(4,1)}), s8[786432]{0:T(1024)(128)(4,1)S(1)}, s32[]{:S(2)}) async-start(s8[9175040]{0:T(1024)(128)(4,1)} %bitcast.341), calls=%async_computation.10 | async-start | bytes 1572864
  599.0 37.8 %slice-start.1 = ((s8[9175040]{0:T(1024)(128)(4,1)}), s8[4194304]{0:T(1024)(128)(4,1)S(1)}, s32[]{:S(2)}) async-start(s8[9175040]{0:T(1024)(128)(4,1)} %bitcast.341), calls=%async_computation.11 | async-start | bytes 8388608
  746.5 705.9 %copy-start.12 = (u32[128]{0:T(128)S(1)}, u32[128]{0:T(128)}, u32[]{:S(2)}) copy-start(u32[128]{0:T(128)} %constant.180) | copy-start | bytes 1540
  746.5 732.6 %copy-start.10 = (f32[1,1,2048]{2,1,0:T(1,128)S(1)}, f32[1,1,2048]{2,1,0:T(1,128)}, u32[]{:S(2)}) copy-start(f32[1,1,2048]{2,1,0:T(1,128)} %get-tuple-element.55) | copy-start | bytes 24580
  1413.8 6.6 collective-permute-start.23
  1415.1 8.3 collective-permute-start.31
  1416.4 18.4 %collective-permute-start.16 = (bf16[16,2560]{1,0:T(8,128)(2,1)S(1)}, bf16[16,2560]{1,0:T(8,128)(2,1)S(1)}, u32[]{:S(2)}, u32[]{:S(2)}) collective-permute-start(bf16[16,2560]{1,0:T(8,128)(2,1)S(1)} %convert.113), channel_id=1, source_target_pairs={{0,1},{1,2},{2,3},{3,4},{4,5},{5,6},{6,7},{7,8},{8,9},{9,10},{10,1... | collective-permute-start | bytes 245768
  1417.7 23.8 %collective-permute-start.17 = (bf16[16,2560]{1,0:T(8,128)(2,1)S(1)}, bf16[16,2560]{1,0:T(8,128)(2,1)S(1)}, u32[]{:S(2)}, u32[]{:S(2)}) collective-permute-start(bf16[16,2560]{1,0:T(8,128)(2,1)S(1)} %convert.113), channel_id=1, source_target_pairs={{0,2},{1,3},{2,4},{3,5},{4,6},{5,7},{6,8},{7,9},{8,10},{9,11},{10,... | collective-permute-start | bytes 245768
  1419.0 28.6 %collective-permute-start.18 = (bf16[16,2560]{1,0:T(8,128)(2,1)S(1)}, bf16[16,2560]{1,0:T(8,128)(2,1)S(1)}, u32[]{:S(2)}, u32[]{:S(2)}) collective-permute-start(bf16[16,2560]{1,0:T(8,128)(2,1)S(1)} %convert.113), channel_id=1, source_target_pairs={{0,3},{1,4},{2,5},{3,6},{4,7},{5,8},{6,9},{7,10},{8,11},{9,12},{10... | collective-permute-start | bytes 245768
  1420.3 28.7 %collective-permute-start.19 = (bf16[16,2560]{1,0:T(8,128)(2,1)S(1)}, bf16[16,2560]{1,0:T(8,128)(2,1)S(1)}, u32[]{:S(2)}, u32[]{:S(2)}) collective-permute-start(bf16[16,2560]{1,0:T(8,128)(2,1)S(1)} %convert.113), channel_id=1, source_target_pairs={{0,4},{1,5},{2,6},{3,7},{4,8},{5,9},{6,10},{7,11},{8,12},{9,13},{1... | collective-permute-start | bytes 245768
  1423.4 9.8 collective-permute-start.7
  1433.2 20.5 %collective-permute-start.20 = (bf16[16,2560]{1,0:T(8,128)(2,1)S(1)}, bf16[16,2560]{1,0:T(8,128)(2,1)S(1)}, u32[]{:S(2)}, u32[]{:S(2)}) collective-permute-start(bf16[16,2560]{1,0:T(8,128)(2,1)S(1)} %convert.113), channel_id=1, source_target_pairs={{0,5},{1,6},{2,7},{3,8},{4,9},{5,10},{6,11},{7,12},{8,13},{9,14},{... | collective-permute-start | bytes 245768
  1434.8 26.5 %collective-permute-start.21 = (bf16[16,2560]{1,0:T(8,128)(2,1)S(1)}, bf16[16,2560]{1,0:T(8,128)(2,1)S(1)}, u32[]{:S(2)}, u32[]{:S(2)}) collective-permute-start(bf16[16,2560]{1,0:T(8,128)(2,1)S(1)} %convert.113), channel_id=1, source_target_pairs={{0,6},{1,7},{2,8},{3,9},{4,10},{5,11},{6,12},{7,13},{8,14},{9,15},... | collective-permute-start | bytes 245768
  1441.5 21.1 %collective-permute-start.22 = (bf16[16,2560]{1,0:T(8,128)(2,1)S(1)}, bf16[16,2560]{1,0:T(8,128)(2,1)S(1)}, u32[]{:S(2)}, u32[]{:S(2)}) collective-permute-start(bf16[16,2560]{1,0:T(8,128)(2,1)S(1)} %convert.113), channel_id=1, source_target_pairs={{0,7},{1,8},{2,9},{3,10},{4,11},{5,12},{6,13},{7,14},{8,15},{9,16}... | collective-permute-start | bytes 245768
  1447.6 19.6 %collective-permute-start.24 = (bf16[16,2560]{1,0:T(8,128)(2,1)S(1)}, bf16[16,2560]{1,0:T(8,128)(2,1)S(1)}, u32[]{:S(2)}, u32[]{:S(2)}) collective-permute-start(bf16[16,2560]{1,0:T(8,128)(2,1)S(1)} %convert.114), channel_id=1, source_target_pairs={{0,1},{1,2},{2,3},{3,4},{4,5},{5,6},{6,7},{7,8},{8,9},{9,10},{10,1... | collective-permute-start | bytes 245768
  1449.1 24.7 %collective-permute-start.25 = (bf16[16,2560]{1,0:T(8,128)(2,1)S(1)}, bf16[16,2560]{1,0:T(8,128)(2,1)S(1)}, u32[]{:S(2)}, u32[]{:S(2)}) collective-permute-start(bf16[16,2560]{1,0:T(8,128)(2,1)S(1)} %convert.114), channel_id=1, source_target_pairs={{0,2},{1,3},{2,4},{3,5},{4,6},{5,7},{6,8},{7,9},{8,10},{9,11},{10,... | collective-permute-start | bytes 245768
  1453.7 42.2 %collective-permute-start.26 = (bf16[16,2560]{1,0:T(8,128)(2,1)S(1)}, bf16[16,2560]{1,0:T(8,128)(2,1)S(1)}, u32[]{:S(2)}, u32[]{:S(2)}) collective-permute-start(bf16[16,2560]{1,0:T(8,128)(2,1)S(1)} %convert.114), channel_id=1, source_target_pairs={{0,3},{1,4},{2,5},{3,6},{4,7},{5,8},{6,9},{7,10},{8,11},{9,12},{10... | collective-permute-start | bytes 245768
  1461.3 37.0 %collective-permute-start.27 = (bf16[16,2560]{1,0:T(8,128)(2,1)S(1)}, bf16[16,2560]{1,0:T(8,128)(2,1)S(1)}, u32[]{:S(2)}, u32[]{:S(2)}) collective-permute-start(bf16[16,2560]{1,0:T(8,128)(2,1)S(1)} %convert.114), channel_id=1, source_target_pairs={{0,4},{1,5},{2,6},{3,7},{4,8},{5,9},{6,10},{7,11},{8,12},{9,13},{1... | collective-permute-start | bytes 245768
  1462.7 39.0 %collective-permute-start.28 = (bf16[16,2560]{1,0:T(8,128)(2,1)S(1)}, bf16[16,2560]{1,0:T(8,128)(2,1)S(1)}, u32[]{:S(2)}, u32[]{:S(2)}) collective-permute-start(bf16[16,2560]{1,0:T(8,128)(2,1)S(1)} %convert.114), channel_id=1, source_target_pairs={{0,5},{1,6},{2,7},{3,8},{4,9},{5,10},{6,11},{7,12},{8,13},{9,14},{... | collective-permute-start | bytes 245768
  1467.2 38.7 %collective-permute-start.29 = (bf16[16,2560]{1,0:T(8,128)(2,1)S(1)}, bf16[16,2560]{1,0:T(8,128)(2,1)S(1)}, u32[]{:S(2)}, u32[]{:S(2)}) collective-permute-start(bf16[16,2560]{1,0:T(8,128)(2,1)S(1)} %convert.114), channel_id=1, source_target_pairs={{0,6},{1,7},{2,8},{3,9},{4,10},{5,11},{6,12},{7,13},{8,14},{9,15},... | collective-permute-start | bytes 245768
  1473.8 33.4 %collective-permute-start.30 = (bf16[16,2560]{1,0:T(8,128)(2,1)S(1)}, bf16[16,2560]{1,0:T(8,128)(2,1)S(1)}, u32[]{:S(2)}, u32[]{:S(2)}) collective-permute-start(bf16[16,2560]{1,0:T(8,128)(2,1)S(1)} %convert.114), channel_id=1, source_target_pairs={{0,7},{1,8},{2,9},{3,10},{4,11},{5,12},{6,13},{7,14},{8,15},{9,16}... | collective-permute-start | bytes 245768
  1495.9 17.2 %collective-permute-start = (bf16[16,2560]{1,0:T(8,128)(2,1)S(1)}, bf16[16,2560]{1,0:T(8,128)(2,1)S(1)}, u32[]{:S(2)}, u32[]{:S(2)}) collective-permute-start(bf16[16,2560]{1,0:T(8,128)(2,1)S(1)} %convert.115), channel_id=1, source_target_pairs={{0,1},{1,2},{2,3},{3,4},{4,5},{5,6},{6,7},{7,8},{8,9},{9,10},{10,1... | collective-permute-start | bytes 245768
  1498.3 21.5 %collective-permute-start.1 = (bf16[16,2560]{1,0:T(8,128)(2,1)S(1)}, bf16[16,2560]{1,0:T(8,128)(2,1)S(1)}, u32[]{:S(2)}, u32[]{:S(2)}) collective-permute-start(bf16[16,2560]{1,0:T(8,128)(2,1)S(1)} %convert.115), channel_id=1, source_target_pairs={{0,2},{1,3},{2,4},{3,5},{4,6},{5,7},{6,8},{7,9},{8,10},{9,11},{10,... | collective-permute-start | bytes 245768
  1501.7 23.6 %collective-permute-start.2 = (bf16[16,2560]{1,0:T(8,128)(2,1)S(1)}, bf16[16,2560]{1,0:T(8,128)(2,1)S(1)}, u32[]{:S(2)}, u32[]{:S(2)}) collective-permute-start(bf16[16,2560]{1,0:T(8,128)(2,1)S(1)} %convert.115), channel_id=1, source_target_pairs={{0,3},{1,4},{2,5},{3,6},{4,7},{5,8},{6,9},{7,10},{8,11},{9,12},{10... | collective-permute-start | bytes 245768
  1505.9 21.1 %collective-permute-start.3 = (bf16[16,2560]{1,0:T(8,128)(2,1)S(1)}, bf16[16,2560]{1,0:T(8,128)(2,1)S(1)}, u32[]{:S(2)}, u32[]{:S(2)}) collective-permute-start(bf16[16,2560]{1,0:T(8,128)(2,1)S(1)} %convert.115), channel_id=1, source_target_pairs={{0,4},{1,5},{2,6},{3,7},{4,8},{5,9},{6,10},{7,11},{8,12},{9,13},{1... | collective-permute-start | bytes 245768
  1507.2 4.3 collective-permute-start.15
  1511.5 18.3 %collective-permute-start.4 = (bf16[16,2560]{1,0:T(8,128)(2,1)S(1)}, bf16[16,2560]{1,0:T(8,128)(2,1)S(1)}, u32[]{:S(2)}, u32[]{:S(2)}) collective-permute-start(bf16[16,2560]{1,0:T(8,128)(2,1)S(1)} %convert.115), channel_id=1, source_target_pairs={{0,5},{1,6},{2,7},{3,8},{4,9},{5,10},{6,11},{7,12},{8,13},{9,14},{... | collective-permute-start | bytes 245768
  1513.1 18.1 %collective-permute-start.5 = (bf16[16,2560]{1,0:T(8,128)(2,1)S(1)}, bf16[16,2560]{1,0:T(8,128)(2,1)S(1)}, u32[]{:S(2)}, u32[]{:S(2)}) collective-permute-start(bf16[16,2560]{1,0:T(8,128)(2,1)S(1)} %convert.115), channel_id=1, source_target_pairs={{0,6},{1,7},{2,8},{3,9},{4,10},{5,11},{6,12},{7,13},{8,14},{9,15},... | collective-permute-start | bytes 245768
  1519.8 13.9 collective-permute-start.6
  1525.4 10.9 collective-permute-start.10
  1527.0 11.5 collective-permute-start.11
  1529.8 15.1 collective-permute-start.12
  1531.2 13.8 collective-permute-start.13
  1533.8 11.2 collective-permute-start.14
  1536.3 8.7 collective-permute-start.8
  1538.5 6.5 collective-permute-start.9
  (8 other events, 73.5 us)
Sparse Core Ops, SparseCore 0:
  10.8 83.0 all-gather.28
  97.4 80.1 all-gather.30
  180.4 68.1 all-gather.32
  251.9 78.4 all-gather.34
  333.7 80.1 all-gather.38
  416.5 68.1 all-gather.36
  580.6 386.0 reduce-scatter.30
  969.2 396.2 reduce-scatter.28
where the time goes:
time: 1570 us; the launch traced here: 1560 us
  blocking collectives  667 us (42%)
  waiting for transfers between devices  346 us (22%)
  matrix products  299 us (19%)
  starting transfers between devices  106 us (7%)
  other arithmetic  83.7 us (5%)
  local copies, waits for them, and re-layouts  39.9 us (3%)
  between operations  16.1 us (1%)
    unnamed x1, blocking collectives  667 us
    squeeze x6, waiting for transfers between devices, stack(): h = layer(h, {name: w[number] for name, w in weights.items()})  342 us
    dot_general x6, matrix products, layer(): up = jnp.dot(a, w['w_up'], preferred_element_type=jnp.float32)  114 us
    unnamed x34, starting transfers between devices  106 us
    dot_general x6, matrix products, layer(): gate = jnp.dot(a, w['w_gate'], preferred_element_type=jnp.float32)  101 us
    dot_general x5, matrix products, matmul(): jnp.dot(a, w, preferred_element_type=jnp.float32).astype(jnp.bfloat16)  83.2 us
    unnamed x8, other arithmetic  65.3 us
    unnamed x46, local copies, waits for them, and re-layouts  34.3 us
  transfers between devices with their start and end apart: 40, of which 8 were waited for; matrix products, arithmetic and copies ran while one was open for 63% of the time, Pallas kernels for 0%

commit v1 on v0

v1 whole, which is shorter than its diff:
```python
import functools

import jax
import jax.numpy as jnp
from jax import lax
from jax.experimental import pallas as pl
from jax.experimental.pallas import tpu as pltpu
from jax.sharding import PartitionSpec as P

MESH = pl.DeviceIdType.MESH
BF, F32 = jnp.bfloat16, jnp.float32
D, FF, LAYERS = 896, 2560, 2
X, Y, Z = 0, 1, 2
GATE, UP, DOWN = 0, 1, 2


def place():
    me = lax.axis_index("dp")
    return lax.axis_index("rep"), (me // 16, (me // 4) % 4, me % 4)


def moved(core, at, dim, by):
    to = [(v + by) % 4 if d == dim else v for d, v in enumerate(at)]
    return core, to[0] * 16 + to[1] * 4 + to[2]


def meet(devices):
    barrier = pltpu.get_barrier_semaphore()
    for device in devices:
        pl.semaphore_signal(barrier, inc=1, device_id=device, device_id_type=MESH)
    pl.semaphore_wait(barrier, len(devices))


GATHER_ORDER = {GATE: (Y, X), UP: (X, Y), DOWN: (X, Y, Z)}
WINDOW = {GATE: (1280, 1280), UP: (1280, 1280), DOWN: (384, 512)}
SHARED = {GATE: (1280, 1280), UP: (1280, 1280), DOWN: (512, 384)}


def gather_kernel(gate, up, down, *refs):
    outs = [refs[0:3], refs[3:6]]
    zb, block, zs, zr, ms, mr, ds, dr, ls = refs[6:]
    core, at = place()
    given = (gate, up, down)
    partner = (1 - core, lax.axis_index("dp"))
    sends = []

    def columns(table, kind, of, part=None):
        step, width = table[kind]
        start = of * step
        if part is not None:
            width //= 2
            start = start + part * width
        return pl.ds(pl.multiple_of(start, 128), width)

    def view(l, kind, p, v, cols):
        order = GATHER_ORDER[kind]
        index = []
        for d in range(3 if kind == DOWN else 2):
            if d in order[:p]:
                index.append(slice(None))
            elif d == order[p]:
                index.append(v)
            else:
                index.append(at[d])
        return outs[l][kind].at[(*index, slice(None), cols)]

    def own(l, kind):
        cols = columns(WINDOW, kind, core)
        return down.at[l, :, cols] if kind == DOWN else block.at[l, kind]

    def send(src, dst, s, r, device):
        copy = pltpu.make_async_remote_copy(src, dst, s, r, device_id=device, device_id_type=MESH)
        copy.start()
        sends.append(copy)

    def arrived(ref, s, r):
        pltpu.make_async_remote_copy(ref, ref, s, r, device_id=partner, device_id_type=MESH).wait_recv()

    def first(l, kind, p):
        dim = GATHER_ORDER[kind][p]
        dst = view(l, kind, p, at[dim], columns(WINDOW, kind, core))
        src = own(l, kind) if p == 0 else dst
        for n, by in enumerate((1, -1)):
            send(src, dst, ms.at[l, kind, p, n], mr.at[l, kind, p, n], moved(core, at, dim, by))

    def relay(l, kind, p):
        dim = GATHER_ORDER[kind][p]
        for n, by in enumerate((1, -1)):
            v = (at[dim] - by) % 4
            arrived(view(l, kind, p, v, columns(WINDOW, kind, core)), ms.at[l, kind, p, n], mr.at[l, kind, p, n])
            half = view(l, kind, p, v, columns(WINDOW, kind, core, n))
            send(half, half, ms.at[l, kind, p, 2 + n], mr.at[l, kind, p, 2 + n], moved(core, at, dim, by))

    def last(l, kind, p):
        v = (at[GATHER_ORDER[kind][p]] + 2) % 4
        for n in range(2):
            half = view(l, kind, p, v, columns(WINDOW, kind, core, n))
            arrived(half, ms.at[l, kind, p, 2 + n], mr.at[l, kind, p, 2 + n])

    def share(l, kind, which, by):
        p = len(GATHER_ORDER[kind]) - 1
        v = (at[GATHER_ORDER[kind][p]] + by) % 4
        ref = view(l, kind, p, v, columns(SHARED, kind, core))
        send(ref, ref, ds.at[l, kind, which], dr.at[l, kind, which], partner)

    def keep(l, kind):
        return pltpu.make_async_copy(
            own(l, kind), view(l, kind, 0, at[GATHER_ORDER[kind][0]], columns(WINDOW, kind, core)), ls.at[l, kind]
        )

    meet([moved(core, at, d, by) for d in (X, Y, Z) for by in (1, 2, -1) if by != 2 or d == Z] + [partner])
    layers = range(LAYERS)
    for l in layers:
        for kind in (GATE, UP):
            cols = columns(WINDOW, kind, core)
            for by in (1, 3, 2):
                send(
                    given[kind].at[l, :, cols],
                    zb.at[l, kind, by - 1],
                    zs.at[l, kind, by - 1],
                    zr.at[l, kind, by - 1],
                    moved(core, at, Z, by),
                )
        first(l, DOWN, 0)
        keep(l, DOWN).start()
    for l in layers:
        for kind in (GATE, UP):
            for n in range(3):
                arrived(zb.at[l, kind, n], zs.at[l, kind, n], zr.at[l, kind, n])
            mine = given[kind][l, :, columns(WINDOW, kind, core)].astype(F32)
            come = [mine, *(zb[l, kind, n].astype(F32) for n in range(3))]
            for z in range(4):

                @pl.when(at[Z] == z)
                def _(z=z, come=come, kind=kind):
                    block[l, kind] = jnp.concatenate([come[(z - row) % 4] for row in range(4)], axis=0).astype(BF)

            first(l, kind, 0)
            keep(l, kind).start()
        relay(l, DOWN, 0)
    for l in layers:
        for kind in (GATE, UP):
            relay(l, kind, 0)
        last(l, DOWN, 0)
        keep(l, DOWN).wait()
        first(l, DOWN, 1)
    for l in layers:
        for kind in (GATE, UP):
            last(l, kind, 0)
            keep(l, kind).wait()
            first(l, kind, 1)
            share(l, kind, 0, 0)
        relay(l, DOWN, 1)
    for l in layers:
        last(l, DOWN, 1)
        first(l, DOWN, 2)
        share(l, DOWN, 0, 0)
        for kind in (GATE, UP):
            relay(l, kind, 1)
            share(l, kind, 1, 1)
            share(l, kind, 2, 3)
    for l in layers:
        for kind in (GATE, UP):
            last(l, kind, 1)
            share(l, kind, 3, 2)
        relay(l, DOWN, 2)
        share(l, DOWN, 1, 1)
        share(l, DOWN, 2, 3)
    for l in layers:
        last(l, DOWN, 2)
        share(l, DOWN, 3, 2)
    for l in layers:
        for kind in (GATE, UP, DOWN):
            p = len(GATHER_ORDER[kind]) - 1
            for which, by in enumerate((0, 1, 3, 2)):
                v = (at[GATHER_ORDER[kind][p]] + by) % 4
                ref = view(l, kind, p, v, columns(SHARED, kind, 1 - core))
                arrived(ref, ds.at[l, kind, which], dr.at[l, kind, which])
    for copy in sends:
        copy.wait_send()


def gather(w_gate, w_up, w_down):
    vmem, anywhere = pl.BlockSpec(memory_space=pltpu.VMEM), pl.BlockSpec(memory_space=pl.ANY)
    wide = jax.ShapeDtypeStruct((4, 4, D // 16, FF), BF)
    tall = jax.ShapeDtypeStruct((4, 4, 4, FF // 64, D), BF)
    dma = pltpu.SemaphoreType.DMA
    outs = pl.pallas_call(
        gather_kernel,
        name="gather",
        out_shape=(wide, wide, tall) * LAYERS,
        in_specs=[vmem] * 3,
        out_specs=(anywhere,) * (3 * LAYERS),
        scratch_shapes=[
            pltpu.VMEM((LAYERS, 2, 3, D // 64, FF // 2), BF),
            pltpu.VMEM((LAYERS, 2, D // 16, FF // 2), BF),
            dma((LAYERS, 2, 3)),
            dma((LAYERS, 2, 3)),
            dma((LAYERS, 3, 3, 4)),
            dma((LAYERS, 3, 3, 4)),
            dma((LAYERS, 3, 4)),
            dma((LAYERS, 3, 4)),
            dma((LAYERS, 3)),
        ],
        compiler_params=pltpu.CompilerParams(collective_id=0, has_side_effects=True),
    )(w_gate, w_up, w_down)
    return [
        (outs[3 * l].reshape(D, FF), outs[3 * l + 1].reshape(D, FF), outs[3 * l + 2].reshape(FF, D))
        for l in range(LAYERS)
    ]


SCATTER_ORDER = {GATE: (X, Y, Z), UP: (Y, X, Z), DOWN: (Z, X, Y)}
SPLIT = {GATE: 1280, UP: 1280, DOWN: 512}
COLS = {GATE: FF, UP: FF, DOWN: D}
STEP = {GATE: 256, UP: 256, DOWN: 128}
BLOCKS = {
    GATE: ((4, 56), (1, 56), (1, 16)),
    UP: ((4, 56), (1, 56), (1, 16)),
    DOWN: ((16, 40), (4, 40), (1, 40)),
}


def scatter_kernel(t_gate, t_up, t_down, o_gate, o_up, o_down, *refs):
    terms, outs = (t_gate, t_up, t_down), (o_gate, o_up, o_down)
    n_buf = 6
    buf = {(k, p): refs[(3 * k + p) * n_buf : (3 * k + p + 1) * n_buf] for k in range(3) for p in range(3)}
    refs = refs[9 * n_buf :]
    wide = {(k, p): refs[2 * k + p - 1] for k in range(3) for p in (1, 2)}
    stage = {(k, p): refs[6 + 2 * k + p - 1] for k in range(3) for p in (1, 2)}
    half = refs[12:14]
    ss, rs = refs[14:16]
    core, at = place()
    sends = []

    def leaving(k, p, v):
        if p == 0:
            if k == GATE:
                return terms[k].at[v]
            if k == UP:
                return terms[k].at[:, v]
            return terms[k].at[:, v]
        return stage[k, p].at[v]

    def held(k, p, v):
        return leaving(k, p, v) if p == 0 else wide[k, p].at[v]

    def part(k, n):
        return pl.ds(0, SPLIT[k]) if n == 0 else pl.ds(SPLIT[k], COLS[k] - SPLIT[k])

    def send(k, p, n, src, dst, by):
        copy = pltpu.make_async_remote_copy(
            src,
            dst,
            ss.at[k, p, n],
            rs.at[k, p, n],
            device_id=moved(core, at, SCATTER_ORDER[k][p], by),
            device_id_type=MESH,
        )
        copy.start()
        sends.append(copy)
        return copy

    def each(k, p, start, width, step):
        def over(body):
            lead = BLOCKS[k][p][0]
            n = width // STEP[k]

            def one(i, carry):
                body(i // n, pl.ds(pl.multiple_of(start + (i % n) * STEP[k], 128), STEP[k]), pl.ds(pl.multiple_of((i % n) * STEP[k], 128), STEP[k]))
                return carry

            lax.fori_loop(0, lead * n, one, 0)

        return over

    transit = {}

    def begin(k, p):
        v = at[SCATTER_ORDER[k][p]]
        from_left, from_right, sum_right, sum_left, left, right = buf[k, p]
        far = leaving(k, p, (v + 2) % 4)
        transit[k, p, 0] = send(k, p, 0, far.at[:, :, part(k, 0)], from_left, 1)
        transit[k, p, 1] = send(k, p, 1, far.at[:, :, part(k, 1)], from_right, -1)
        transit[k, p, 2] = send(
            k, p, 2, leaving(k, p, (v + 1) % 4).at[:, :, part(k, 1)], left.at[:, :, part(k, 1)], 1
        )
        transit[k, p, 3] = send(
            k, p, 3, leaving(k, p, (v + 3) % 4).at[:, :, part(k, 0)], right.at[:, :, part(k, 0)], -1
        )

    def middle(k, p):
        v = at[SCATTER_ORDER[k][p]]
        from_left, from_right, sum_right, sum_left, left, right = buf[k, p]
        for n, by, come, total, dst in ((0, 1, from_left, sum_right, left), (1, -1, from_right, sum_left, right)):
            transit[k, p, n].wait_recv()
            mine = held(k, p, (v + by) % 4)
            start, width = (0, SPLIT[k]) if n == 0 else (SPLIT[k], COLS[k] - SPLIT[k])

            @each(k, p, start, width, None)
            def _(i, whole, here, mine=mine, come=come, total=total):
                total[i, :, here] = (mine[i, :, whole].astype(F32) + come[i, :, here].astype(F32)).astype(BF)

            transit[k, p, 4 + n] = send(k, p, 4 + n, total, dst.at[:, :, part(k, n)], by)

    def end(k, p):
        v = at[SCATTER_ORDER[k][p]]
        left, right = buf[k, p][4:]
        for n in range(2, 6):
            transit[k, p, n].wait_recv()
        mine = held(k, p, v)

        @each(k, p, 0, COLS[k], None)
        def _(i, cols, _):
            total = mine[i, :, cols].astype(F32) + left[i, :, cols].astype(F32) + right[i, :, cols].astype(F32)
            if p == 2:
                if k == DOWN:
                    outs[k][:, cols] = total.astype(BF)
                else:
                    outs[k][:, cols] = total[:14].astype(BF)
            elif k != DOWN and p == 1:
                for z in range(4):
                    rows = jnp.concatenate([total[14 * z : 14 * z + 14], jnp.zeros((2, STEP[k]), F32)], axis=0)
                    wide[k, 2][z, 0, :, cols] = rows
                    stage[k, 2][z, 0, :, cols] = rows.astype(BF)
            elif k != DOWN or p == 1:
                wide[k, p + 1][i, 0, :, cols] = total
                stage[k, p + 1][i, 0, :, cols] = total.astype(BF)
            else:
                wide[k, 1][i // 4, i % 4, :, cols] = total
                stage[k, 1][i // 4, i % 4, :, cols] = total.astype(BF)

    meet([moved(core, at, d, by) for d in (X, Y, Z) for by in (1, -1)])
    kinds = (DOWN, GATE, UP)
    for k in kinds:
        begin(k, 0)
    for p in range(3):
        for k in kinds:
            middle(k, p)
        for k in kinds:
            end(k, p)
            if p < 2:
                begin(k, p + 1)
    for copy in sends:
        copy.wait_send()


def scatter(t_gate, t_up, t_down, number):
    vmem = pl.BlockSpec(memory_space=pltpu.VMEM)
    scratch = []
    for k in range(3):
        for lead, rows in BLOCKS[k]:
            one, other = SPLIT[k], COLS[k] - SPLIT[k]
            for cols in (one, other, one, other, COLS[k], COLS[k]):
                scratch.append(pltpu.VMEM((lead, rows, cols), BF))
    for kind in (F32, BF):
        for k in range(3):
            for lead, rows in BLOCKS[k][1:]:
                scratch.append(pltpu.VMEM((4, lead, rows, COLS[k]), kind))
    scratch += [pltpu.VMEM((8, 128), BF)] * 2
    scratch += [pltpu.SemaphoreType.DMA((3, 3, 6))] * 2
    return pl.pallas_call(
        scatter_kernel,
        name=f"scatter_{number}",
        out_shape=(
            jax.ShapeDtypeStruct((D // 64, FF), BF),
            jax.ShapeDtypeStruct((D // 64, FF), BF),
            jax.ShapeDtypeStruct((FF // 64, D), BF),
        ),
        in_specs=[vmem] * 3,
        out_specs=(vmem,) * 3,
        scratch_shapes=scratch,
        compiler_params=pltpu.CompilerParams(
            collective_id=1, has_side_effects=True, vmem_limit_bytes=60 * 1024 * 1024
        ),
    )(t_gate.reshape(4, 4, 56, FF), t_up.reshape(4, 4, 56, FF), t_down.reshape(16, 4, 40, D))


def dot(a, b, over=((1,), (0,))):
    return lax.dot_general(a, b, (over, ((), ())), preferred_element_type=F32)


def norm(h):
    wide = h.astype(F32)
    scale = lax.rsqrt(jnp.mean(wide**2, -1, keepdims=True) + 1e-6)
    return (wide * scale).astype(BF), scale


def norm_back(h, scale, by_a):
    wide, by = h.astype(F32), by_a.astype(F32)
    inner = jnp.mean(by * wide, -1, keepdims=True)
    return (by * scale - wide * (scale * scale * scale * inner)).astype(BF)


def gated(gate, up):
    return (jax.nn.silu(gate) * up).astype(BF)


def back(h, a, scale, gate, up, act, by_y, weights):
    w_gate, w_up, w_down = weights
    by_act = dot(by_y, w_down, ((1,), (1,))).astype(BF)
    t_down = dot(act, by_y, ((0,), (0,))).astype(BF)
    sig = jax.nn.sigmoid(gate)
    by_act = by_act.astype(F32)
    by_up = (by_act * (gate * sig)).astype(BF)
    by_gate = (by_act * up * (sig * (1 + gate * (1 - sig)))).astype(BF)
    t_gate = dot(a, by_gate, ((0,), (0,))).astype(BF)
    t_up = dot(a, by_up, ((0,), (0,))).astype(BF)
    by_a = dot(by_gate, w_gate, ((1,), (1,))).astype(BF) + dot(by_up, w_up, ((1,), (1,))).astype(BF)
    return by_y + norm_back(h, scale, by_a), (t_gate, t_up, t_down)


def local(x, dy, w_gate, w_up, w_down):
    x, dy = x[0], dy[0]
    first, second = gather(w_gate, w_up, w_down)
    a0, s0 = norm(x)
    g0, u0 = dot(a0, first[0]), dot(a0, first[1])
    act0 = gated(g0, u0)
    h = x + dot(act0, first[2]).astype(BF)
    a1, s1 = norm(h)
    g1, u1 = dot(a1, second[0]), dot(a1, second[1])
    by_h, terms = back(h, a1, s1, g1, u1, gated(g1, u1), dy, second)
    of_second = scatter(*terms, 1)
    by_x, terms = back(x, a0, s0, g0, u0, act0, by_h, first)
    of_first = scatter(*terms, 0)
    return (by_x[None], *(jnp.stack(pair) for pair in zip(of_first, of_second)))


def solution(mesh):
    tokens, rows = P(("rep", "dp")), P(None, "dp", None)
    return jax.shard_map(
        local,
        mesh=mesh,
        in_specs=(tokens, tokens, rows, rows, rows),
        out_specs=(tokens, *([P("rep", "dp", None)] * 3)),
        check_vma=False,
    )
```

time: 1570 us -> 600 us (0.38)
  blocking collectives: 667 us -> 0 us
  waiting for transfers between devices: 346 us -> 0 us
  Pallas kernels: 0 us -> 248 us
  starting transfers between devices: 106 us -> 0 us
  other arithmetic: 83.7 us -> 17.6 us
  local copies, waits for them, and re-layouts: 39.9 us -> 21.4 us
    unnamed x1 -> x0, blocking collectives: 667 us -> none
    squeeze x6 -> x0, waiting for transfers between devices: 342 us -> none  [stack(): h = layer(h, {name: w[number] for name, w in weights.items()})]
    pallas_call x0 -> x3, Pallas kernels: none -> 248 us  [the longest x2 157 us: scatter(): pl.pallas_call(scatter_kernel, name=f'scatter_{number}', out_shape=(jax.S...]
    unnamed x34 -> x0, starting transfers between devices: 106 us -> none
    unnamed x8 -> x0, other arithmetic: 65.3 us -> none
    unnamed x46 -> x53, local copies, waits for them, and re-layouts: 34.3 us -> 21.4 us
  transfers between devices with their start and end apart: 40 -> 0, of which waited for: 8 -> 0; matrix products, arithmetic and copies ran while one was open for 63% -> 0% of each run, Pallas kernels for 0% -> 0%
where the time goes in v1:
time: 600 us; the launch traced here: 590 us
  matrix products  302 us (50%)
  Pallas kernels  248 us (41%)
  local copies, waits for them, and re-layouts  21.4 us (4%)
  other arithmetic  17.6 us (3%)
    dot_general x17, matrix products, dot(): return lax.dot_general(a, b, (over, ((), ())), preferred_element_type=F32)  302 us
    pallas_call x2, Pallas kernels, scatter(): pl.pallas_call(scatter_kernel, name=f'scatter_{number}', out_shape=(jax.S...  157 us
    pallas_call x1, Pallas kernels, gather(): pl.pallas_call(gather_kernel, name='gather', out_shape=(wide, wide, tall)...  90.7 us
    unnamed x53, local copies, waits for them, and re-layouts  21.4 us

profile of v1, /device:TPU:0, one launch (start us, length us, event | category | flops | bytes accessed | tf_op | source)
XLA Modules:
  0.0 590.1 jit_solution(11240882642654972870)
XLA Ops:
  0.6 0.0 copy-start.9
  0.6 0.0 copy-start.10
  0.7 6.1 %copy.12 = bf16[1,2048,896]{1,2,0:T(8,128)(2,1)} copy(bf16[1,2048,896]{2,1,0:T(8,128)(2,1)} %param.5) | data formatting | bytes 7340032 | tf_op args[0]
  6.8 2.8 fusion.13
  9.6 0.0 copy-done.9
  9.6 0.0 copy-start.16
  9.6 0.7 copy.10.gate
  10.3 0.0 copy-done.13
  10.3 0.7 copy.11.up
  11.0 90.7 %gather.1 = (bf16[4,4,56,2560]{3,2,1,0:T(8,128)(2,1)}, bf16[4,4,56,2560]{3,2,1,0:T(8,128)(2,1)}, bf16[4,4,4,40,896]{4,3,2,1,0:T(8,128)(2,1)}, bf16[4,4,56,2560]{...) custom-call(bf16[2,14,2560]{2,1,0:T(8,128)(2,1)} %copy.10.gate, ...), custom_call_target="tpu_custom_call" | custom-call | tf_op jit(solution)/shard_map/gather/pallas_call | solution.py:188
  101.6 0.0 copy-start.5
  101.7 18.3 %fusion.37 = f32[2048,2560]{0,1:T(8,128)} fusion(bf16[896,2560]{1,0:T(8,128)(2,1)} %bitcast.90, bf16[1,2048,896]{2,1,0:T(8,128)(2,1)} %param.5, f32[2048]{0:T(1024)S(1)} %add_rsqrt_fusion.1), kind=kOutput, calls=%fused_computation.58 | convolution fusion | flops 9400745984 | bytes 29237248 | tf_op jit(solution)/shard_map/dot_general | solution.py:380
  119.9 25.0 %multiply_convert_fusion.1 = (bf16[2048,2560]{0,1:T(8,128)(2,1)}, f32[2048,2560]{0,1:T(8,128)}) fusion(f32[2048,2560]{0,1:T(8,128)} %fusion.37, bf16[896,2560]{1,0:T(8,128)(2,1)} %bitcast.88, bf16[1,2048,896]{2,1,0:T(8,128)(2,1)S(1)} %copy-done.5, f32[2048]{0:T(1024)S(1)} %add_rsqrt_fusion.1), kind=kOutput, calls=%fused_computation.13 | convolution fusion | flops 9432203264 | bytes 60694528 | tf_op jit(solution)/shard_map/dot_general | solution.py:380
  144.9 0.0 copy-done
  144.9 14.8 %fusion.16 = (f32[2048]{0:T(1024)S(1)}, bf16[2048,896]{0,1:T(8,128)(2,1)S(1)}) fusion(bf16[2048,2560]{0,1:T(8,128)(2,1)} %get-tuple-element.36, bf16[2560,896]{1,0:T(8,128)(2,1)} %bitcast.92, bf16[1,2048,896]{1,2,0:T(8,128)(2,1)S(1)} %copy-done), kind=kOutput, calls=%fused_computation.36 | convolution fusion | flops 9404413952 | bytes 22421504 | tf_op jit(solution)/shard_map/dot_general | solution.py:380
  159.7 0.0 copy-start.18
  159.7 14.4 %fusion.33 = f32[2048,2560]{0,1:T(8,128)} fusion(bf16[896,2560]{1,0:T(8,128)(2,1)S(1)} %bitcast.95, bf16[2048,896]{0,1:T(8,128)(2,1)S(1)} %get-tuple-element.39, f32[2048]{0:T(1024)S(1)} %add_rsqrt_fusion), kind=kOutput, calls=%fused_computation.56 | convolution fusion | flops 9400745984 | bytes 29237248 | tf_op jit(solution)/shard_map/dot_general | solution.py:380
  174.1 17.5 %fusion.31 = f32[2048,2560]{0,1:T(8,128)} fusion(bf16[896,2560]{1,0:T(8,128)(2,1)} %bitcast.96, bf16[2048,896]{0,1:T(8,128)(2,1)S(1)} %get-tuple-element.39, f32[2048]{0:T(1024)S(1)} %add_rsqrt_fusion), kind=kOutput, calls=%fused_computation.55 | convolution fusion | flops 9400745984 | bytes 29237248 | tf_op jit(solution)/shard_map/dot_general | solution.py:380
  191.6 28.9 %fusion.5 = (bf16[2048,2560]{0,1:T(8,128)(2,1)}, bf16[2048,2560]{0,1:T(8,128)(2,1)}) fusion(f32[2048,2560]{0,1:T(8,128)} %fusion.31, f32[2048,2560]{0,1:T(8,128)} %fusion.33, bf16[2560,896]{1,0:T(8,128)(2,1)} %bitcast.98, bf16[1,2048,896]{2,1,0:T(8,128)(2,1)S(1)} %copy-done.6), kind=kOutput, calls=%fused_computation.9 | convolution fusion | flops 9473884160 | bytes 71172096 | tf_op jit(solution)/shard_map/dot_general | solution.py:380
  220.5 14.0 %fusion.42 = bf16[2048,896]{0,1:T(8,128)(2,1)S(1)} fusion(bf16[896,2560]{1,0:T(8,128)(2,1)} %bitcast.97, bf16[2048,2560]{0,1:T(8,128)(2,1)} %get-tuple-element.35), kind=kOutput, calls=%fused_computation.69 | convolution fusion | flops 9395240960 | bytes 18743296 | tf_op jit(solution)/shard_map/dot_general | solution.py:380
  234.5 13.7 %fusion.18 = (f32[2048]{0:T(1024)S(1)}, bf16[2048,896]{0,1:T(8,128)(2,1)}) fusion(bf16[2048,896]{0,1:T(8,128)(2,1)S(1)} %get-tuple-element.39, bf16[2048,896]{0,1:T(8,128)(2,1)S(1)} %fusion.42, bf16[896,2560]{1,0:T(8,128)(2,1)} %bitcast.94, bf16[2048,2560]{0,1:T(8,128)(2,1)S(1)} %copy-done.22), kind=kOutput, calls=%fused_computation.38 | convolution fusion | flops 9406248960 | bytes 26091520 | tf_op jit(solution)/shard_map/dot_general | solution.py:380
  248.2 6.1 %copy.9 = bf16[1,2048,896]{1,2,0:T(8,128)(2,1)} copy(bf16[1,2048,896]{2,1,0:T(8,128)(2,1)} %param.6) | data formatting | bytes 7340032 | tf_op args[1]
  254.3 6.8 %fusion.23 = bf16[2048,896]{0,1:T(8,128)(2,1)S(1)} fusion(bf16[2048,896]{0,1:T(8,128)(2,1)} %copy-done.7, bf16[2048,896]{0,1:T(8,128)(2,1)} %get-tuple-element.41, bf16[1,2048,896]{1,2,0:T(8,128)(2,1)} %copy.9, f32[2048]{0:T(1024)S(1)} %fusion.39, f32[2048]{0:T(1024)S(1)} %add_rsqrt_fusion), kind=kLoop, calls=%fused_computation.49 | loop fusion | flops 12845056 | bytes 14696448 | tf_op jit(solution)/shard_map/add | solution.py:410
  261.2 16.6 %convolution_convert_fusion.2 = bf16[2560,896]{1,0:T(8,128)(2,1)} fusion(bf16[2048,2560]{0,1:T(8,128)(2,1)} %get-tuple-element.36, bf16[2048,896]{0,1:T(8,128)(2,1)S(1)} %fusion.23), kind=kOutput, calls=%fused_computation.40 | convolution fusion | flops 9397534720 | bytes 18743296 | tf_op jit(solution)/shard_map/dot_general | solution.py:380
  277.8 31.6 %fusion.2 = (bf16[2048,2560]{0,1:T(8,128)(2,1)}, bf16[2048,2560]{0,1:T(8,128)(2,1)}) fusion(f32[2048,2560]{0,1:T(8,128)} %fusion.37, f32[2048,2560]{0,1:T(8,128)} %get-tuple-element.37, bf16[2560,896]{1,0:T(8,128)(2,1)} %bitcast.93, bf16[2048,896]{0,1:T(8,128)(2,1)} %copy-done.3), kind=kOutput, calls=%fused_computation.4 | convolution fusion | flops 9473884160 | bytes 71172096 | tf_op jit(solution)/shard_map/dot_general | solution.py:380
  309.4 0.0 copy-done.17
  309.4 16.8 %convolution_convert_fusion.6 = bf16[896,2560]{1,0:T(8,128)(2,1)} fusion(bf16[2048,2560]{0,1:T(8,128)(2,1)} %get-tuple-element.33, bf16[1,2048,896]{1,2,0:T(8,128)(2,1)} %copy.12, f32[2048]{0:T(1024)S(1)} %copy-done.17), kind=kOutput, calls=%fused_computation.45 | convolution fusion | flops 9403039744 | bytes 18751488 | tf_op jit(solution)/shard_map/dot_general | solution.py:380
  326.2 11.4 %convolution_convert_fusion.5 = bf16[896,2560]{1,0:T(8,128)(2,1)} fusion(bf16[2048,2560]{0,1:T(8,128)(2,1)S(1)} %copy-done.21, bf16[1,2048,896]{1,2,0:T(8,128)(2,1)S(1)} %copy-done.1, f32[2048]{0:T(1024)S(1)} %copy-done.17), kind=kOutput, calls=%fused_computation.44 | convolution fusion | flops 9403039744 | bytes 18751488 | tf_op jit(solution)/shard_map/dot_general | solution.py:380
  337.6 81.4 %scatter_0.1 = (bf16[14,2560]{1,0:T(8,128)(2,1)}, bf16[14,2560]{1,0:T(8,128)(2,1)}, bf16[40,896]{1,0:T(8,128)(2,1)}) custom-call(bf16[4,4,56,2560]{3,2,1,0:T(8,128)(2,1)} %bitcast.80, bf16[4,4,56,2560]{3,2,1,0:T(8,128)(2,1)} %bitcast.81, bf16[16,4,40,896]{3,2,1,0:T(8,128)(2,1)} %bitcast.76), custom_call_target="tpu_custom_call" | custom-call | tf_op jit(solution)/shard_map/scatter_0/pallas_call | solution.py:362
  419.0 0.0 copy-start.19
  419.0 21.4 %fusion.19 = bf16[2560,896]{1,0:T(8,128)(2,1)} fusion(f32[2048,2560]{0,1:T(8,128)} %fusion.33, bf16[1,2048,896]{2,1,0:T(8,128)(2,1)} %param.6, f32[2048,2560]{0,1:T(8,128)} %fusion.31), kind=kOutput, calls=%fused_computation.41 | convolution fusion | flops 9428992000 | bytes 50200576 | tf_op jit(solution)/shard_map/dot_general | solution.py:380
  440.5 15.1 %convolution_convert_fusion.3 = bf16[896,2560]{1,0:T(8,128)(2,1)} fusion(bf16[2048,2560]{0,1:T(8,128)(2,1)} %get-tuple-element.34, bf16[2048,896]{0,1:T(8,128)(2,1)} %copy-done.7, f32[2048]{0:T(1024)S(1)} %copy-done.19), kind=kOutput, calls=%fused_computation.42 | convolution fusion | flops 9403039744 | bytes 18751488 | tf_op jit(solution)/shard_map/dot_general | solution.py:380
  455.5 0.0 copy-done.8
  455.6 14.0 %convolution_convert_fusion.4 = bf16[896,2560]{1,0:T(8,128)(2,1)} fusion(bf16[2048,2560]{0,1:T(8,128)(2,1)} %get-tuple-element.35, bf16[2048,896]{0,1:T(8,128)(2,1)S(1)} %copy-done.8, f32[2048]{0:T(1024)S(1)} %copy-done.19), kind=kOutput, calls=%fused_computation.43 | convolution fusion | flops 9403039744 | bytes 18751488 | tf_op jit(solution)/shard_map/dot_general | solution.py:380
  469.6 76.0 %scatter_1.1 = (bf16[14,2560]{1,0:T(8,128)(2,1)}, bf16[14,2560]{1,0:T(8,128)(2,1)}, bf16[40,896]{1,0:T(8,128)(2,1)}) custom-call(bf16[4,4,56,2560]{3,2,1,0:T(8,128)(2,1)} %bitcast.79, bf16[4,4,56,2560]{3,2,1,0:T(8,128)(2,1)} %bitcast.78, bf16[16,4,40,896]{3,2,1,0:T(8,128)(2,1)} %bitcast.77), custom_call_target="tpu_custom_call" | custom-call | tf_op jit(solution)/shard_map/scatter_1/pallas_call | solution.py:362
  545.6 1.6 pad_maximum_fusion.2
  547.1 0.9 pad_maximum_fusion.1
  548.1 0.8 copy.26
  548.9 0.9 pad_maximum_fusion
  549.8 0.8 copy.25
  550.6 13.8 %fusion.43 = bf16[2048,896]{0,1:T(8,128)(2,1)S(1)} fusion(bf16[896,2560]{1,0:T(8,128)(2,1)} %bitcast.91, bf16[2048,2560]{0,1:T(8,128)(2,1)} %get-tuple-element.33), kind=kOutput, calls=%fused_computation.70 | convolution fusion | flops 9395240960 | bytes 18743296 | tf_op jit(solution)/shard_map/dot_general | solution.py:380
  564.4 0.0 copy-done.2
  564.4 0.0 copy-start.14
  564.5 0.0 copy-start.4
  564.5 14.6 %fusion.14 = (f32[2048]{0:T(1024)S(1)}, bf16[2048,896]{0,1:T(8,128)(2,1)S(1)}) fusion(bf16[1,2048,896]{1,2,0:T(8,128)(2,1)S(1)} %copy-done.2, bf16[2048,896]{0,1:T(8,128)(2,1)S(1)} %fusion.43, bf16[896,2560]{1,0:T(8,128)(2,1)} %bitcast.89, bf16[2048,2560]{0,1:T(8,128)(2,1)} %get-tuple-element.32), kind=kOutput, calls=%fused_computation.34 | convolution fusion | flops 9406248960 | bytes 26091520 | tf_op jit(solution)/shard_map/dot_general | solution.py:380
  579.0 0.0 copy-done.14
  579.1 4.5 fusion.22
  583.6 6.0 %copy.24 = bf16[1,2048,896]{2,1,0:T(8,128)(2,1)} copy(bf16[1,2048,896]{1,2,0:T(8,128)(2,1)} %fusion.22) | data formatting | bytes 7340032
  (35 shorter events, 0.1 us)
Async XLA Ops:
  0.6 9.0 %copy-start.9 = (bf16[2,14,2560]{2,0,1:T(2,128)(2,1)S(1)}, bf16[2,14,2560]{2,0,1:T(2,128)(2,1)}, u32[]{:S(2)}) copy-start(bf16[2,14,2560]{2,0,1:T(2,128)(2,1)} %param.7) | copy-start | bytes 430084
  0.6 9.7 %copy-start.10 = (bf16[2,14,2560]{2,0,1:T(2,128)(2,1)S(1)}, bf16[2,14,2560]{2,0,1:T(2,128)(2,1)}, u32[]{:S(2)}) copy-start(bf16[2,14,2560]{2,0,1:T(2,128)(2,1)} %param.8) | copy-start | bytes 430084
  9.6 0.7 copy-start.13
  9.6 110.3 %copy-start.16 = (f32[2048]{0:T(1024)}, f32[2048]{0:T(1024)S(1)}, u32[]{:S(2)}) copy-start(f32[2048]{0:T(1024)S(1)} %add_rsqrt_fusion.1) | copy-start | bytes 24580
  101.6 18.3 %copy-start.5 = (bf16[1,2048,896]{2,1,0:T(8,128)(2,1)S(1)}, bf16[1,2048,896]{2,1,0:T(8,128)(2,1)}, u32[]{:S(2)}) copy-start(bf16[1,2048,896]{2,1,0:T(8,128)(2,1)} %param.5) | copy-start | bytes 11010052
  119.9 25.0 %copy-start = (bf16[1,2048,896]{1,2,0:T(8,128)(2,1)S(1)}, bf16[1,2048,896]{1,2,0:T(8,128)(2,1)}, u32[]{:S(2)}) copy-start(bf16[1,2048,896]{1,2,0:T(8,128)(2,1)} %copy.12) | copy-start | bytes 11010052
  144.9 14.8 %copy-start.20 = (bf16[4,4,56,2560]{3,2,1,0:T(8,128)(2,1)S(1)}, bf16[4,4,56,2560]{3,2,1,0:T(8,128)(2,1)}, u32[]{:S(2)}) copy-start(bf16[4,4,56,2560]{3,2,1,0:T(8,128)(2,1)} %get-tuple-element.20) | copy-start | bytes 13762564
  159.7 74.8 %copy-start.7 = (bf16[2048,896]{0,1:T(8,128)(2,1)}, bf16[2048,896]{0,1:T(8,128)(2,1)S(1)}, u32[]{:S(2)}) copy-start(bf16[2048,896]{0,1:T(8,128)(2,1)S(1)} %get-tuple-element.39) | copy-start | bytes 11010052
  159.7 94.6 %copy-start.18 = (f32[2048]{0:T(1024)}, f32[2048]{0:T(1024)S(1)}, u32[]{:S(2)}) copy-start(f32[2048]{0:T(1024)S(1)} %add_rsqrt_fusion) | copy-start | bytes 24580
  174.1 17.5 %copy-start.6 = (bf16[1,2048,896]{2,1,0:T(8,128)(2,1)S(1)}, bf16[1,2048,896]{2,1,0:T(8,128)(2,1)}, u32[]{:S(2)}) copy-start(bf16[1,2048,896]{2,1,0:T(8,128)(2,1)} %param.6) | copy-start | bytes 11010052
  220.5 14.0 %copy-start.22 = (bf16[2048,2560]{0,1:T(8,128)(2,1)S(1)}, bf16[2048,2560]{0,1:T(8,128)(2,1)}, u32[]{:S(2)}) copy-start(bf16[2048,2560]{0,1:T(8,128)(2,1)} %get-tuple-element.34) | copy-start | bytes 31457284
  261.2 16.6 %copy-start.3 = (bf16[2048,896]{0,1:T(8,128)(2,1)}, bf16[2048,896]{0,1:T(8,128)(2,1)S(1)}, u32[]{:S(2)}) copy-start(bf16[2048,896]{0,1:T(8,128)(2,1)S(1)} %fusion.23) | copy-start | bytes 11010052
  277.8 31.6 %copy-start.17 = (f32[2048]{0:T(1024)S(1)}, f32[2048]{0:T(1024)}, u32[]{:S(2)}) copy-start(f32[2048]{0:T(1024)} %copy-done.16) | copy-start | bytes 24580
  309.4 16.8 %copy-start.1 = (bf16[1,2048,896]{1,2,0:T(8,128)(2,1)S(1)}, bf16[1,2048,896]{1,2,0:T(8,128)(2,1)}, u32[]{:S(2)}) copy-start(bf16[1,2048,896]{1,2,0:T(8,128)(2,1)} %copy.12) | copy-start | bytes 11010052
  309.4 16.8 %copy-start.21 = (bf16[2048,2560]{0,1:T(8,128)(2,1)S(1)}, bf16[2048,2560]{0,1:T(8,128)(2,1)}, u32[]{:S(2)}) copy-start(bf16[2048,2560]{0,1:T(8,128)(2,1)} %get-tuple-element.32) | copy-start | bytes 31457284
  419.0 21.4 %copy-start.19 = (f32[2048]{0:T(1024)S(1)}, f32[2048]{0:T(1024)}, u32[]{:S(2)}) copy-start(f32[2048]{0:T(1024)} %copy-done.18) | copy-start | bytes 24580
  440.5 15.1 %copy-start.8 = (bf16[2048,896]{0,1:T(8,128)(2,1)S(1)}, bf16[2048,896]{0,1:T(8,128)(2,1)}, u32[]{:S(2)}) copy-start(bf16[2048,896]{0,1:T(8,128)(2,1)} %copy-done.7) | copy-start | bytes 11010052
  469.6 76.0 %copy-start.15 = (bf16[40,896]{1,0:T(8,128)(2,1)S(1)}, bf16[40,896]{1,0:T(8,128)(2,1)}, u32[]{:S(2)}) copy-start(bf16[40,896]{1,0:T(8,128)(2,1)} %get-tuple-element.26) | copy-start | bytes 215044
  469.6 77.6 %copy-start.12 = (bf16[14,2560]{1,0:T(8,128)(2,1)S(1)}, bf16[14,2560]{1,0:T(8,128)(2,1)}, u32[]{:S(2)}) copy-start(bf16[14,2560]{1,0:T(8,128)(2,1)} %get-tuple-element.24) | copy-start | bytes 215044
  469.6 79.3 %copy-start.11 = (bf16[14,2560]{1,0:T(8,128)(2,1)S(1)}, bf16[14,2560]{1,0:T(8,128)(2,1)}, u32[]{:S(2)}) copy-start(bf16[14,2560]{1,0:T(8,128)(2,1)} %get-tuple-element.22) | copy-start | bytes 215044
  550.6 13.8 %copy-start.2 = (bf16[1,2048,896]{1,2,0:T(8,128)(2,1)S(1)}, bf16[1,2048,896]{1,2,0:T(8,128)(2,1)}, u32[]{:S(2)}) copy-start(bf16[1,2048,896]{1,2,0:T(8,128)(2,1)} %copy.12) | copy-start | bytes 11010052
  564.4 14.6 %copy-start.14 = (f32[2048]{0:T(1024)S(1)}, f32[2048]{0:T(1024)}, u32[]{:S(2)}) copy-start(f32[2048]{0:T(1024)} %copy-done.13) | copy-start | bytes 24580
  564.5 14.6 %copy-start.4 = (bf16[2048,896]{0,1:T(8,128)(2,1)S(1)}, bf16[2048,896]{0,1:T(8,128)(2,1)}, u32[]{:S(2)}) copy-start(bf16[2048,896]{0,1:T(8,128)(2,1)} %copy-done.3) | copy-start | bytes 11010052

commit v2 on v0

v2 whole, which is shorter than its diff:
```python
import functools

import jax
import jax.numpy as jnp
from jax import lax
from jax.experimental import pallas as pl
from jax.experimental.pallas import tpu as pltpu
from jax.sharding import PartitionSpec as P

MESH = pl.DeviceIdType.MESH
BF, F32 = jnp.bfloat16, jnp.float32
D, FF, LAYERS = 896, 2560, 2
X, Y, Z = 0, 1, 2
GATE, UP, DOWN = 0, 1, 2


def place():
    me = lax.axis_index("dp")
    return lax.axis_index("rep"), (me // 16, (me // 4) % 4, me % 4)


def moved(core, at, dim, by):
    to = [(v + by) % 4 if d == dim else v for d, v in enumerate(at)]
    return core, to[0] * 16 + to[1] * 4 + to[2]


def meet(devices):
    barrier = pltpu.get_barrier_semaphore()
    for device in devices:
        pl.semaphore_signal(barrier, inc=1, device_id=device, device_id_type=MESH)
    pl.semaphore_wait(barrier, len(devices))


BYTES = 63 * 1024 * 1024
GATHER_ORDER = {GATE: (Y, X), UP: (X, Y), DOWN: (X, Y, Z)}
WINDOW = {GATE: (1280, 1280), UP: (1280, 1280), DOWN: (384, 512)}
SHARED = {GATE: (1280, 1280), UP: (1280, 1280), DOWN: (512, 384)}


def gather_plan(l, given, outs, refs):
    zb, block, zs, zr, ms, mr, ds, dr, ls = refs
    core, at = place()
    partner = (1 - core, lax.axis_index("dp"))

    def columns(table, kind, of, part=None):
        step, width = table[kind]
        start = of * step
        if part is not None:
            width //= 2
            start = start + part * width
        return pl.ds(pl.multiple_of(start, 128), width)

    def view(kind, p, by, cols):
        order = GATHER_ORDER[kind]
        index = []
        for d in range(3 if kind == DOWN else 2):
            if d in order[:p]:
                index.append(slice(None))
            elif d == order[p]:
                index.append((at[d] + by) % 4)
            else:
                index.append(at[d])
        return outs[kind].at[(*index, slice(None), cols)]

    def mine(kind):
        cols = columns(WINDOW, kind, core)
        return given[kind].at[l, :, cols] if kind == DOWN else block.at[kind]

    def remote(src, dst, s, r, device):
        return pltpu.make_async_remote_copy(src, dst, s, r, device_id=device, device_id_type=MESH)

    def near(kind, by):
        src, sem = given[kind].at[l, :, columns(WINDOW, kind, core)], (kind, by - 1)
        return remote(src, zb.at[sem], zs.at[sem], zr.at[sem], moved(core, at, Z, by))

    def first(kind, p, n):
        dst = view(kind, p, 0, columns(WINDOW, kind, core))
        to = moved(core, at, GATHER_ORDER[kind][p], (1, -1)[n])
        return remote(mine(kind) if p == 0 else dst, dst, ms.at[kind, p, n], mr.at[kind, p, n], to)

    def relay(kind, p, n):
        by = (1, -1)[n]
        half = view(kind, p, -by, columns(WINDOW, kind, core, n))
        to = moved(core, at, GATHER_ORDER[kind][p], by)
        return remote(half, half, ms.at[kind, p, 2 + n], mr.at[kind, p, 2 + n], to)

    SHARES = (0, 1, 3, 2)

    def share(kind, which):
        ref = view(kind, len(GATHER_ORDER[kind]) - 1, SHARES[which], columns(SHARED, kind, core))
        return remote(ref, ref, ds.at[kind, which], dr.at[kind, which], partner)

    def keep(kind):
        return pltpu.make_async_copy(mine(kind), view(kind, 0, 0, columns(WINDOW, kind, core)), ls.at[kind])

    def arrived(ref, s, r):
        remote(ref, ref, s, r, partner).wait_recv()

    def start_first(kind, p):
        for n in range(2):
            first(kind, p, n).start()

    def pass_on(kind, p):
        for n in range(2):
            ref = view(kind, p, -(1, -1)[n], columns(WINDOW, kind, core))
            arrived(ref, ms.at[kind, p, n], mr.at[kind, p, n])
            relay(kind, p, n).start()

    def finish(kind, p):
        for n in range(2):
            arrived(view(kind, p, 2, columns(WINDOW, kind, core, n)), ms.at[kind, p, 2 + n], mr.at[kind, p, 2 + n])

    def stage0():
        meet([moved(core, at, d, by) for d in (X, Y, Z) for by in (1, 2, -1) if by != 2 or d == Z] + [partner])
        for kind in (GATE, UP):
            for by in (1, 3, 2):
                near(kind, by).start()
        start_first(DOWN, 0)
        keep(DOWN).start()

    def stage1():
        for kind in (GATE, UP):
            for n in range(3):
                arrived(zb.at[kind, n], zs.at[kind, n], zr.at[kind, n])
            come = [given[kind][l, :, columns(WINDOW, kind, core)].astype(F32)]
            come += [zb[kind, n].astype(F32) for n in range(3)]
            for z in range(4):

                @pl.when(at[Z] == z)
                def _(z=z, come=come, kind=kind):
                    block[kind] = jnp.concatenate([come[(z - row) % 4] for row in range(4)], axis=0).astype(BF)

            start_first(kind, 0)
            keep(kind).start()
        pass_on(DOWN, 0)

    def stage2():
        for kind in (GATE, UP):
            pass_on(kind, 0)
        finish(DOWN, 0)
        keep(DOWN).wait()
        start_first(DOWN, 1)

    def stage3():
        for kind in (GATE, UP):
            finish(kind, 0)
            keep(kind).wait()
            start_first(kind, 1)
            share(kind, 0).start()
        pass_on(DOWN, 1)

    def stage4():
        finish(DOWN, 1)
        start_first(DOWN, 2)
        share(DOWN, 0).start()

    def stage5():
        for kind in (GATE, UP):
            pass_on(kind, 1)
            share(kind, 1).start()
            share(kind, 2).start()

    def stage6():
        pass_on(DOWN, 2)
        share(DOWN, 1).start()
        share(DOWN, 2).start()

    def stage7():
        for kind in (GATE, UP):
            finish(kind, 1)
            share(kind, 3).start()

    def stage8():
        finish(DOWN, 2)
        share(DOWN, 3).start()
        for kind in (GATE, UP, DOWN):
            for which in range(4):
                p = len(GATHER_ORDER[kind]) - 1
                ref = view(kind, p, SHARES[which], columns(SHARED, kind, 1 - core))
                arrived(ref, ds.at[kind, which], dr.at[kind, which])
        for kind in (GATE, UP):
            for by in (1, 3, 2):
                near(kind, by).wait_send()
        for kind in (GATE, UP, DOWN):
            for p in range(len(GATHER_ORDER[kind])):
                for n in range(2):
                    first(kind, p, n).wait_send()
                    relay(kind, p, n).wait_send()
            for which in range(4):
                share(kind, which).wait_send()

    return [stage0, stage1, stage2, stage3, stage4, stage5, stage6, stage7, stage8]


def gather_scratch():
    dma = pltpu.SemaphoreType.DMA
    return [
        pltpu.VMEM((2, 3, D // 64, FF // 2), BF),
        pltpu.VMEM((2, D // 16, FF // 2), BF),
        dma((2, 3)),
        dma((2, 3)),
        dma((3, 3, 4)),
        dma((3, 3, 4)),
        dma((3, 4)),
        dma((3, 4)),
        dma((3,)),
    ]


VMEM, ANYWHERE = pl.BlockSpec(memory_space=pltpu.VMEM), pl.BlockSpec(memory_space=pl.ANY)


def gathered():
    wide = jax.ShapeDtypeStruct((4, 4, D // 16, FF), BF)
    return wide, wide, jax.ShapeDtypeStruct((4, 4, 4, FF // 64, D), BF)


def matrices(gate, up, down):
    return gate.reshape(D, FF), up.reshape(D, FF), down.reshape(FF, D)


def gather(shards):
    def kernel(*refs):
        for stage in gather_plan(0, refs[:3], refs[3:6], refs[6:]):
            stage()

    return matrices(
        *pl.pallas_call(
            kernel,
            name="gather",
            out_shape=gathered(),
            in_specs=[VMEM] * 3,
            out_specs=(ANYWHERE,) * 3,
            scratch_shapes=gather_scratch(),
            compiler_params=pltpu.CompilerParams(collective_id=0, has_side_effects=True),
        )(*shards)
    )


SCATTER_ORDER = {GATE: (X, Y, Z), UP: (Y, X, Z), DOWN: (Z, X, Y)}
SPLIT = {GATE: 1280, UP: 1280, DOWN: 512}
COLS = {GATE: FF, UP: FF, DOWN: D}
STEP = {GATE: 256, UP: 256, DOWN: 128}
BLOCKS = {
    GATE: ((4, 56), (1, 56), (1, 16)),
    UP: ((4, 56), (1, 56), (1, 16)),
    DOWN: ((16, 40), (4, 40), (1, 40)),
}
KINDS = (DOWN, GATE, UP)


def scatter_plan(terms, outs, refs):
    refs = list(refs)
    buf = {(k, p): [refs.pop(0) for _ in range(4)] for k in range(3) for p in range(3)}
    wide = {(k, p): refs.pop(0) for k in range(3) for p in (1, 2)}
    stage = {(k, p): refs.pop(0) for k in range(3) for p in (1, 2)}
    own = {k: [refs.pop(0) for _ in range(3)] for k in range(3)}
    ss, rs, ls = refs
    core, at = place()

    def block(k, p, by):
        v = (at[SCATTER_ORDER[k][p]] + by) % 4
        if p:
            return stage[k, p].at[v]
        return terms[k].at[v] if k == GATE else terms[k].at[:, v]

    def part(k, n):
        return pl.ds(0, SPLIT[k]) if n == 0 else pl.ds(SPLIT[k], COLS[k] - SPLIT[k])

    def flow(k, p, n):
        from_left, from_right, left, right = buf[k, p]
        src, dst = {
            0: lambda: (block(k, p, 2).at[:, :, part(k, 0)], from_left),
            1: lambda: (block(k, p, 2).at[:, :, part(k, 1)], from_right),
            2: lambda: (block(k, p, 1).at[:, :, part(k, 1)], left.at[:, :, part(k, 1)]),
            3: lambda: (block(k, p, -1).at[:, :, part(k, 0)], right.at[:, :, part(k, 0)]),
            4: lambda: (from_left, left.at[:, :, part(k, 0)]),
            5: lambda: (from_right, right.at[:, :, part(k, 1)]),
        }[n]()
        to = moved(core, at, SCATTER_ORDER[k][p], (1, -1)[n % 2])
        sems = ss.at[k, p, n], rs.at[k, p, n]
        return pltpu.make_async_remote_copy(src, dst, *sems, device_id=to, device_id_type=MESH)

    def load(k, n):
        src = (lambda: block(k, 0, 1).at[:, :, part(k, 0)], lambda: block(k, 0, -1).at[:, :, part(k, 1)], lambda: block(k, 0, 0))[n]()
        return pltpu.make_async_copy(src, own[k][n], ls.at[k, n])

    def each(k, p, width, body):
        count = width // STEP[k]

        def one(i, carry):
            body(i // count, (i % count) * STEP[k])
            return carry

        lax.fori_loop(0, BLOCKS[k][p][0] * count, one, 0)

    def here(k, start):
        return pl.ds(pl.multiple_of(start, 128), STEP[k])

    def begin(k, p):
        for n in range(4):
            flow(k, p, n).start()
        if p == 0:
            for n in range(3):
                load(k, n).start()

    def middle(k, p):
        for n in range(2):
            flow(k, p, n).wait_recv()
            if p == 0:
                load(k, n).wait()
            come, before = buf[k, p][n], 0 if p == 0 or n == 0 else SPLIT[k]
            mine = own[k][n] if p == 0 else wide[k, p].at[(at[SCATTER_ORDER[k][p]] + (1, -1)[n]) % 4]

            def add(i, start, mine=mine, come=come, before=before):
                cols = here(k, start)
                come[i, :, cols] = (mine[i, :, here(k, start + before)].astype(F32) + come[i, :, cols].astype(F32)).astype(BF)

            each(k, p, SPLIT[k] if n == 0 else COLS[k] - SPLIT[k], add)
            flow(k, p, 4 + n).start()

    def end(k, p):
        left, right = buf[k, p][2:]
        for n in range(2, 6):
            flow(k, p, n).wait_recv()
        if p == 0:
            load(k, 2).wait()
        mine = own[k][2] if p == 0 else wide[k, p].at[at[SCATTER_ORDER[k][p]]]

        def add(i, start):
            cols = here(k, start)
            total = mine[i, :, cols].astype(F32) + left[i, :, cols].astype(F32) + right[i, :, cols].astype(F32)
            if p == 2:
                outs[k][:, cols] = total[: outs[k].shape[0]].astype(BF)
            elif k != DOWN and p == 1:
                for z in range(4):
                    rows = jnp.concatenate([total[14 * z : 14 * z + 14], jnp.zeros((2, STEP[k]), F32)], axis=0)
                    wide[k, 2][z, 0, :, cols] = rows
                    stage[k, 2][z, 0, :, cols] = rows.astype(BF)
            else:
                at_row = (i, 0) if k != DOWN or p == 1 else (i // 4, i % 4)
                wide[k, p + 1][(*at_row, slice(None), cols)] = total
                stage[k, p + 1][(*at_row, slice(None), cols)] = total.astype(BF)

        each(k, p, COLS[k], add)
        if p < 2:
            begin(k, p + 1)

    def enter():
        meet([moved(core, at, d, by) for d in (X, Y, Z) for by in (1, -1)])
        for k in KINDS:
            begin(k, 0)

    def leave():
        for k in KINDS:
            for p in range(3):
                for n in range(6):
                    flow(k, p, n).wait_send()

    stages = [enter]
    for p in range(3):
        stages += [functools.partial(middle, k, p) for k in KINDS]
        stages += [functools.partial(end, k, p) for k in KINDS]
    return [*stages, leave]


def scatter_scratch():
    scratch = []
    for k in range(3):
        for lead, rows in BLOCKS[k]:
            for cols in (SPLIT[k], COLS[k] - SPLIT[k], COLS[k], COLS[k]):
                scratch.append(pltpu.VMEM((lead, rows, cols), BF))
    for kind in (F32, BF):
        for k in range(3):
            for lead, rows in BLOCKS[k][1:]:
                scratch.append(pltpu.VMEM((4, lead, rows, COLS[k]), kind))
    for k in range(3):
        lead, rows = BLOCKS[k][0]
        for cols in (SPLIT[k], COLS[k] - SPLIT[k], COLS[k]):
            scratch.append(pltpu.VMEM((lead, rows, cols), BF))
    dma = pltpu.SemaphoreType.DMA
    return [*scratch, dma((3, 3, 6)), dma((3, 3, 6)), dma((3, 3))]


def scattered():
    wide = jax.ShapeDtypeStruct((D // 64, FF), BF)
    return wide, wide, jax.ShapeDtypeStruct((FF // 64, D), BF)


def blocked(t_gate, t_up, t_down):
    return t_gate.reshape(4, 4, 56, FF), t_up.reshape(4, 4, 56, FF), t_down.reshape(16, 4, 40, D)


def scatter(terms):
    def kernel(*refs):
        for stage in scatter_plan(refs[:3], refs[3:6], refs[6:]):
            stage()

    return pl.pallas_call(
        kernel,
        name="scatter",
        out_shape=scattered(),
        in_specs=[ANYWHERE] * 3,
        out_specs=(VMEM,) * 3,
        scratch_shapes=scatter_scratch(),
        compiler_params=pltpu.CompilerParams(collective_id=1, has_side_effects=True, vmem_limit_bytes=BYTES),
    )(*blocked(*terms))


TOKENS, CHUNK = 2048, 512
GATHER_AT = ((0, 0), (0, 3), (1, 0), (1, 3), (2, 0), (3, 3), (4, 3), (6, 3), (7, 3))
SCATTER_AT = (
    (0, 0),
    *((1, 3), (2, 0), (2, 0)),
    *((4, 0), (4, 3), (5, 0)),
    *((5, 3), (5, 3), (5, 3)),
    *((6, 0), (6, 3), (6, 3)),
    *((7, 0), (7, 0), (7, 0)),
    *((7, 3), (7, 3), (7, 3)),
    (7, 5),
)


def run(stages, places, number):
    for stage, (tile, chunk) in zip(stages, places, strict=True):
        if chunk == number:
            pl.when(pl.program_id(0) == tile)(stage)

ROWS = ((1,), (1,))
FIRST = ((0,), (0,))


def dot(a, b, over=((1,), (0,))):
    return lax.dot_general(a, b, (over, ((), ())), preferred_element_type=F32)


def norm(h):
    wide = h.astype(F32)
    scale = lax.rsqrt(jnp.mean(wide * wide, -1, keepdims=True) + 1e-6)
    return (wide * scale).astype(BF), scale


def chunks():
    return [slice(j, j + CHUNK) for j in range(0, FF, CHUNK)]


def forward_kernel(h_ref, gate_ref, up_ref, down_ref, *refs):
    out_ref = refs[3]
    plan = gather_plan(1, refs[:3], refs[4:7], refs[7:])
    h = h_ref[...]
    a, _ = norm(h)
    total = None
    for number, cols in enumerate(chunks()):
        run(plan, GATHER_AT, number)
        gate, up = dot(a, gate_ref[:, cols]), dot(a, up_ref[:, cols])
        act = (gate * jax.nn.sigmoid(gate) * up).astype(BF)
        more = dot(act, down_ref[cols, :])
        total = more if total is None else total + more
    run(plan, GATHER_AT, len(chunks()))
    out_ref[...] = h + total.astype(BF)


def backward_kernel(hosts, h_ref, by_ref, gate_ref, up_ref, down_ref, *refs):
    if hosts:
        terms, refs = refs[:3], refs[3:]
    by_h_ref, a_ref, act_ref, by_gate_ref, by_up_ref, *refs = refs
    plan, places = (scatter_plan(terms, refs[:3], refs[3:]), SCATTER_AT) if hosts else ((), ())
    h, by = h_ref[...], by_ref[...]
    a, scale = norm(h)
    a_ref[...] = a
    total = None
    for number, cols in enumerate(chunks()):
        run(plan, places, number)
        gate, up = dot(a, gate_ref[:, cols]), dot(a, up_ref[:, cols])
        by_act = dot(by, down_ref[cols, :], ROWS).astype(BF).astype(F32)
        sig = jax.nn.sigmoid(gate)
        silu = gate * sig
        act_ref[:, cols] = (silu * up).astype(BF)
        by_up = (by_act * silu).astype(BF)
        by_gate = (by_act * up * (sig + silu * (1 - sig))).astype(BF)
        by_up_ref[:, cols] = by_up
        by_gate_ref[:, cols] = by_gate
        more = dot(by_gate, gate_ref[:, cols], ROWS) + dot(by_up, up_ref[:, cols], ROWS)
        total = more if total is None else total + more
    run(plan, places, len(chunks()))
    by_a = total.astype(BF).astype(F32)
    wide = h.astype(F32)
    inner = jnp.mean(by_a * wide, -1, keepdims=True)
    by_h_ref[...] = by + (by_a * scale - wide * (scale * scale * scale * inner)).astype(BF)


def weights_kernel(a_ref, by_ref, act_ref, by_gate_ref, by_up_ref, t_gate_ref, t_up_ref, t_down_ref, turned):
    @pl.when(pl.program_id(0) == 0)
    def _():
        turned[...] = a_ref[...].T

    t_down_ref[...] = dot(act_ref[...], by_ref[...], FIRST).astype(BF)
    t_gate_ref[...] = dot(turned[...], by_gate_ref[...]).astype(BF)
    t_up_ref[...] = dot(turned[...], by_up_ref[...]).astype(BF)


def whole(shape):
    return pl.BlockSpec(shape, lambda i: (0, 0), pipeline_mode=pl.Buffered(1))


def of_tokens(tile, cols):
    return pl.BlockSpec((tile, cols), lambda i: (i, 0))


def cost(matmuls):
    return pl.CostEstimate(flops=matmuls * 2 * TOKENS * D * FF, transcendentals=0, bytes_accessed=40_000_000)


def shaped(*shape):
    return jax.ShapeDtypeStruct(shape, BF)


BIG = pltpu.CompilerParams(vmem_limit_bytes=BYTES)
WEIGHTS = [whole((D, FF)), whole((D, FF)), whole((FF, D))]


def forward(h, weights, shards):
    tile = TOKENS // 8
    h, *others = pl.pallas_call(
        forward_kernel,
        name="forward",
        grid=(TOKENS // tile,),
        out_shape=(shaped(TOKENS, D), *gathered()),
        in_specs=[of_tokens(tile, D), *WEIGHTS, *[VMEM] * 3],
        out_specs=(of_tokens(tile, D), *[ANYWHERE] * 3),
        scratch_shapes=gather_scratch(),
        compiler_params=pltpu.CompilerParams(collective_id=2, has_side_effects=True, vmem_limit_bytes=BYTES),
        cost_estimate=cost(3),
    )(h, *weights, *shards)
    return h, matrices(*others)


def back(h, by, weights, number, terms=()):
    tile = TOKENS // 8 if terms else TOKENS // 4
    params = BIG
    if terms:
        params = pltpu.CompilerParams(collective_id=3, has_side_effects=True, vmem_limit_bytes=BYTES)
    by_h, a, act, by_gate, by_up, *sums = pl.pallas_call(
        functools.partial(backward_kernel, bool(terms)),
        name=f"backward_{number}",
        grid=(TOKENS // tile,),
        out_shape=(shaped(TOKENS, D), shaped(TOKENS, D), *[shaped(TOKENS, FF)] * 3, *(scattered() if terms else ())),
        in_specs=[of_tokens(tile, D), of_tokens(tile, D), *WEIGHTS, *([ANYWHERE] * len(terms))],
        out_specs=(
            *[of_tokens(tile, D)] * 2,
            *[of_tokens(tile, FF)] * 3,
            *([VMEM] * len(terms)),
        ),
        scratch_shapes=scatter_scratch() if terms else (),
        compiler_params=params,
        cost_estimate=cost(5),
    )(h, by, *weights, *(blocked(*terms) if terms else ()))
    side = pl.BlockSpec((TOKENS, CHUNK), lambda i: (0, i))
    terms = pl.pallas_call(
        weights_kernel,
        name=f"weights_{number}",
        grid=(FF // CHUNK,),
        out_shape=(shaped(D, FF), shaped(D, FF), shaped(FF, D)),
        in_specs=[whole((TOKENS, D)), whole((TOKENS, D)), side, side, side],
        out_specs=(
            pl.BlockSpec((D, CHUNK), lambda i: (0, i)),
            pl.BlockSpec((D, CHUNK), lambda i: (0, i)),
            pl.BlockSpec((CHUNK, D), lambda i: (i, 0)),
        ),
        scratch_shapes=[pltpu.VMEM((D, TOKENS), BF)],
        compiler_params=BIG,
        cost_estimate=cost(3),
    )(a, by, act, by_gate, by_up)
    return by_h, terms, sums


def local(x, dy, *shards):
    x, dy = x[0], dy[0]
    first = gather(shards)
    h, second = forward(x, first, shards)
    by_h, terms, _ = back(h, dy, second, 1)
    by_x, terms, of_second = back(x, by_h, first, 0, terms)
    of_first = scatter(terms)
    return (by_x[None], *(jnp.stack(pair) for pair in zip(of_first, of_second)))


def solution(mesh):
    tokens, rows = P(("rep", "dp")), P(None, "dp", None)
    return jax.shard_map(
        local,
        mesh=mesh,
        in_specs=(tokens, tokens, rows, rows, rows),
        out_specs=(tokens, *([P("rep", "dp", None)] * 3)),
        check_vma=False,
    )
```

time: 1570 us -> 464 us (0.30)
  blocking collectives: 667 us -> 0 us
  Pallas kernels: 0 us -> 450 us
  waiting for transfers between devices: 346 us -> 0 us
  matrix products: 299 us -> 0 us
  starting transfers between devices: 106 us -> 0 us
  other arithmetic: 83.7 us -> 3.38 us
  local copies, waits for them, and re-layouts: 39.9 us -> 8.97 us
    unnamed x1 -> x0, blocking collectives: 667 us -> none
    pallas_call x0 -> x7, Pallas kernels: none -> 450 us  [the longest x2 165 us: back(): pl.pallas_call(functools.partial(backward_kernel, bool(terms)), name=f'ba...]
    squeeze x6 -> x0, waiting for transfers between devices: 342 us -> none  [stack(): h = layer(h, {name: w[number] for name, w in weights.items()})]
    dot_general x17 -> x0, matrix products: 299 us -> none  [the longest x6 114 us: layer(): up = jnp.dot(a, w['w_up'], preferred_element_type=jnp.float32)]
    unnamed x34 -> x0, starting transfers between devices: 106 us -> none
    unnamed x8 -> x0, other arithmetic: 65.3 us -> none
    unnamed x46 -> x11, local copies, waits for them, and re-layouts: 34.3 us -> 8.97 us
  transfers between devices with their start and end apart: 40 -> 0, of which waited for: 8 -> 0; matrix products, arithmetic and copies ran while one was open for 63% -> 0% of each run, Pallas kernels for 0% -> 0%
where the time goes in v2:
time: 464 us; the launch traced here: 463 us
  Pallas kernels  450 us (97%)
  local copies, waits for them, and re-layouts  8.97 us (2%)
    pallas_call x2, Pallas kernels, back(): pl.pallas_call(functools.partial(backward_kernel, bool(terms)), name=f'ba...  165 us
    pallas_call x2, Pallas kernels, back(): pl.pallas_call(weights_kernel, name=f'weights_{number}', grid=(FF // CHUN...  78.2 us
    pallas_call x1, Pallas kernels, forward(): pl.pallas_call(forward_kernel, name='forward', grid=(TOKENS // tile,), ou...  75.1 us
    pallas_call x1, Pallas kernels, scatter(): pl.pallas_call(kernel, name='scatter', out_shape=scattered(), in_specs=[A...  69.9 us
    pallas_call x1, Pallas kernels, gather(): pl.pallas_call(kernel, name='gather', out_shape=gathered(), in_specs=[VME...  62.3 us

profile of v2, /device:TPU:0, one launch (start us, length us, event | category | flops | bytes accessed | tf_op | source)
XLA Modules:
  0.0 463.4 jit_solution(9992427900817837416)
XLA Ops:
  0.6 1.6 copy.9.refs_0_
  2.2 1.6 copy.10.refs_1_
  3.8 62.3 %gather.1 = (bf16[4,4,56,2560]{3,2,1,0:T(8,128)(2,1)}, bf16[4,4,56,2560]{3,2,1,0:T(8,128)(2,1)}, bf16[4,4,4,40,896]{4,3,2,1,0:T(8,128)(2,1)}) custom-call(bf16[2,14,2560]{2,1,0:T(8,128)(2,1)} %copy.9.refs_0_, bf16[2,14,2560]{2,1,0:T(8,128)(2,1)} %copy.10.refs_1_, bf16[2,40,896]{2,1,0:T(8,128)(2,1)} %refs_2_.3), custom_call_target="tpu_custom_call" | custom-call | tf_op jit(solution)/shard_map/gather/pallas_call | solution.py:228
  66.1 75.1 %forward.1 = (bf16[2048,896]{1,0:T(8,128)(2,1)}, bf16[4,4,56,2560]{3,2,1,0:T(8,128)(2,1)}, bf16[4,4,56,2560]{3,2,1,0:T(8,128)(2,1)}, bf16[4,4,4,40,896]{4,3,2,1,0:T(8,128)(2,1)}) custom-call(bf16[2048,896]{1,0:T(8,128)(2,1)} %bitcast.39, bf16[896,2560]{1,0:T(8,128)(2,1)} %bitcast.31, bf16[896,2560]{1,0:T(8,128)(2,1)} %bitcast.33, ...), custom_call_target="tpu_custom_call" | custom-call | flops 28185722880 | bytes 40000000 | tf_op jit(solution)/shard_map/forward/pallas_call | solution.py:524
  141.2 68.6 %backward_1.1 = (bf16[2048,896]{1,0:T(8,128)(2,1)}, bf16[2048,896]{1,0:T(8,128)(2,1)}, bf16[2048,2560]{1,0:T(8,128)(2,1)}, bf16[2048,2560]{1,0:T(8,128)(2,1)}, bf16[2048,2560]{1,0:T(8,128)(2,1)}) custom-call(bf16[2048,896]{1,0:T(8,128)(2,1)} %get-tuple-element.36.h_ref, bf16[2048,896]{1,0:T(8,128)(2,1)} %bitcast.37, bf16[896,2560]{1,0:T(8,128)(2,1)} %bitcast.44, ...), custom_call_target="tpu_custom_call" | custom-call | flops 46976204800 | bytes 40000000 | tf_op jit(solution)/shard_map/backward_1/pallas_call | solution.py:543
  209.8 39.1 %weights_1.1 = (bf16[896,2560]{1,0:T(8,128)(2,1)}, bf16[896,2560]{1,0:T(8,128)(2,1)}, bf16[2560,896]{1,0:T(8,128)(2,1)}) custom-call(bf16[2048,896]{1,0:T(8,128)(2,1)} %get-tuple-element.41.a_ref, bf16[2048,896]{1,0:T(8,128)(2,1)} %bitcast.38, bf16[2048,2560]{1,0:T(8,128)(2,1)} %get-tuple-element.42.act_ref, ...), custom_call_target="tpu_custom_call" | custom-call | flops 28185722880 | bytes 40000000 | tf_op jit(solution)/shard_map/weights_1/pallas_call | solution.py:559
  248.9 96.3 %backward_0.1 = (bf16[2048,896]{1,0:T(8,128)(2,1)}, bf16[2048,896]{1,0:T(8,128)(2,1)}, bf16[2048,2560]{1,0:T(8,128)(2,1)}, bf16[2048,2560]{1,0:T(8,128)(2,1)}, b...) custom-call(bf16[2048,896]{1,0:T(8,128)(2,1)} %bitcast.40, ...), custom_call_target="tpu_custom_call" | custom-call | flops 46976204800 | bytes 40000000 | tf_op jit(solution)/shard_map/backward_0/pallas_call | solution.py:543
  345.2 39.1 %weights_0.1 = (bf16[896,2560]{1,0:T(8,128)(2,1)}, bf16[896,2560]{1,0:T(8,128)(2,1)}, bf16[2560,896]{1,0:T(8,128)(2,1)}) custom-call(bf16[2048,896]{1,0:T(8,128)(2,1)} %get-tuple-element.49.a_ref, bf16[2048,896]{1,0:T(8,128)(2,1)} %get-tuple-element.40.by_ref, bf16[2048,2560]{1,0:T(8,128)(2,1)} %get-tuple-element.50.act_ref, ...), custom_call_target="tpu_custom_call" | custom-call | flops 28185722880 | bytes 40000000 | tf_op jit(solution)/shard_map/weights_0/pallas_call | solution.py:559
  384.3 0.0 copy-start.1
  384.3 0.0 copy-start
  384.3 0.0 copy-start.2
  384.3 69.9 %scatter.1 = (bf16[14,2560]{1,0:T(8,128)(2,1)}, bf16[14,2560]{1,0:T(8,128)(2,1)}, bf16[40,896]{1,0:T(8,128)(2,1)}) custom-call(bf16[4,4,56,2560]{3,2,1,0:T(8,128)(2,1)} %bitcast.21, bf16[4,4,56,2560]{3,2,1,0:T(8,128)(2,1)} %bitcast.22, bf16[16,4,40,896]{3,2,1,0:T(8,128)(2,1)} %bitcast.23), custom_call_target="tpu_custom_call" | custom-call | tf_op jit(solution)/shard_map/scatter/pallas_call | solution.py:399
  454.2 0.0 copy-done.1
  454.2 0.9 pad_maximum_fusion
  455.1 0.8 copy.13
  455.9 0.0 copy-done
  455.9 0.9 pad_maximum_fusion.1
  456.8 0.8 copy.14
  457.6 0.0 copy-done.2
  457.6 1.6 pad_maximum_fusion.2
  459.2 4.2 copy.16
Async XLA Ops:
  384.3 69.9 %copy-start.1 = (bf16[14,2560]{1,0:T(8,128)(2,1)S(1)}, bf16[14,2560]{1,0:T(8,128)(2,1)}, u32[]{:S(2)}) copy-start(bf16[14,2560]{1,0:T(8,128)(2,1)} %get-tuple-element.57) | copy-start | bytes 215044
  384.3 71.6 %copy-start = (bf16[14,2560]{1,0:T(8,128)(2,1)S(1)}, bf16[14,2560]{1,0:T(8,128)(2,1)}, u32[]{:S(2)}) copy-start(bf16[14,2560]{1,0:T(8,128)(2,1)} %get-tuple-element.59) | copy-start | bytes 215044
  384.3 73.3 %copy-start.2 = (bf16[40,896]{1,0:T(8,128)(2,1)S(1)}, bf16[40,896]{1,0:T(8,128)(2,1)}, u32[]{:S(2)}) copy-start(bf16[40,896]{1,0:T(8,128)(2,1)} %get-tuple-element.61) | copy-start | bytes 215044

commit v3 on v2

v3 whole, which is shorter than its diff:
```python
import functools

import jax
import jax.numpy as jnp
from jax import lax
from jax.experimental import pallas as pl
from jax.experimental.pallas import tpu as pltpu
from jax.sharding import PartitionSpec as P

MESH = pl.DeviceIdType.MESH
BF, F32 = jnp.bfloat16, jnp.float32
D, FF, LAYERS = 896, 2560, 2
X, Y, Z = 0, 1, 2
GATE, UP, DOWN = 0, 1, 2


def place():
    me = lax.axis_index("dp")
    return lax.axis_index("rep"), (me // 16, (me // 4) % 4, me % 4)


def moved(core, at, dim, by):
    to = [(v + by) % 4 if d == dim else v for d, v in enumerate(at)]
    return core, to[0] * 16 + to[1] * 4 + to[2]


def meet(devices):
    barrier = pltpu.get_barrier_semaphore()
    for device in devices:
        pl.semaphore_signal(barrier, inc=1, device_id=device, device_id_type=MESH)
    pl.semaphore_wait(barrier, len(devices))


BYTES = 63 * 1024 * 1024
GATHER_ORDER = {GATE: (Y, X), UP: (X, Y), DOWN: (X, Y, Z)}
WINDOW = {GATE: (1280, 1280), UP: (1280, 1280), DOWN: (384, 512)}
SHARED = {GATE: (1280, 1280), UP: (1280, 1280), DOWN: (512, 384)}


def gather_plan(l, given, outs, refs, meeting=True):
    zb, block, zs, zr, ms, mr, ds, dr, ls = refs
    core, at = place()
    partner = (1 - core, lax.axis_index("dp"))

    def columns(table, kind, of, part=None):
        step, width = table[kind]
        start = of * step
        if part is not None:
            width //= 2
            start = start + part * width
        return pl.ds(pl.multiple_of(start, 128), width)

    def view(kind, p, by, cols):
        order = GATHER_ORDER[kind]
        index = []
        for d in range(3 if kind == DOWN else 2):
            if d in order[:p]:
                index.append(slice(None))
            elif d == order[p]:
                index.append((at[d] + by) % 4)
            else:
                index.append(at[d])
        return outs[kind].at[(*index, slice(None), cols)]

    def mine(kind):
        cols = columns(WINDOW, kind, core)
        return given[kind].at[l, :, cols] if kind == DOWN else block.at[kind]

    def remote(src, dst, s, r, device):
        return pltpu.make_async_remote_copy(src, dst, s, r, device_id=device, device_id_type=MESH)

    def near(kind, by):
        src, sem = given[kind].at[l, :, columns(WINDOW, kind, core)], (kind, by - 1)
        return remote(src, zb.at[sem], zs.at[sem], zr.at[sem], moved(core, at, Z, by))

    def first(kind, p, n, part):
        dst = view(kind, p, 0, columns(WINDOW, kind, core, part))
        width = WINDOW[kind][1] // 2
        src = dst
        if p == 0 and kind == DOWN:
            src = given[kind].at[l, :, columns(WINDOW, kind, core, part)]
        elif p == 0:
            src = block.at[kind, :, pl.ds(part * width, width)]
        to = moved(core, at, GATHER_ORDER[kind][p], (1, -1)[n])
        which = n if part == n else 4 + n
        return remote(src, dst, ms.at[kind, p, which], mr.at[kind, p, which], to)

    def relay(kind, p, n):
        by = (1, -1)[n]
        half = view(kind, p, -by, columns(WINDOW, kind, core, n))
        to = moved(core, at, GATHER_ORDER[kind][p], by)
        return remote(half, half, ms.at[kind, p, 2 + n], mr.at[kind, p, 2 + n], to)

    SHARES = (0, 1, 3, 2)

    def share(kind, which):
        ref = view(kind, len(GATHER_ORDER[kind]) - 1, SHARES[which], columns(SHARED, kind, core))
        return remote(ref, ref, ds.at[kind, which], dr.at[kind, which], partner)

    def keep(kind):
        return pltpu.make_async_copy(mine(kind), view(kind, 0, 0, columns(WINDOW, kind, core)), ls.at[kind])

    def arrived(ref, s, r):
        remote(ref, ref, s, r, partner).wait_recv()

    def start_first(kind, p):
        for part in (0, 1):
            for n in range(2):
                first(kind, p, n, n if part == 0 else 1 - n).start()

    def pass_on(kind, p):
        for n in range(2):
            ref = view(kind, p, -(1, -1)[n], columns(WINDOW, kind, core, n))
            arrived(ref, ms.at[kind, p, n], mr.at[kind, p, n])
            relay(kind, p, n).start()

    def rest(kind, p):
        for n in range(2):
            ref = view(kind, p, -(1, -1)[n], columns(WINDOW, kind, core, 1 - n))
            arrived(ref, ms.at[kind, p, 4 + n], mr.at[kind, p, 4 + n])

    def finish(kind, p):
        for n in range(2):
            arrived(view(kind, p, 2, columns(WINDOW, kind, core, n)), ms.at[kind, p, 2 + n], mr.at[kind, p, 2 + n])

    def stage0():
        if meeting:
            meet([moved(core, at, d, by) for d in (X, Y, Z) for by in (1, 2, -1) if by != 2 or d == Z] + [partner])
        for kind in (GATE, UP):
            for by in (1, 3, 2):
                near(kind, by).start()
        start_first(DOWN, 0)
        keep(DOWN).start()

    def stage1():
        for kind in (GATE, UP):
            for n in range(3):
                arrived(zb.at[kind, n], zs.at[kind, n], zr.at[kind, n])
            come = [given[kind][l, :, columns(WINDOW, kind, core)].astype(F32)]
            come += [zb[kind, n].astype(F32) for n in range(3)]
            for z in range(4):

                @pl.when(at[Z] == z)
                def _(z=z, come=come, kind=kind):
                    block[kind] = jnp.concatenate([come[(z - row) % 4] for row in range(4)], axis=0).astype(BF)

            start_first(kind, 0)
            keep(kind).start()
        pass_on(DOWN, 0)

    def stage2():
        for kind in (GATE, UP):
            pass_on(kind, 0)
        rest(DOWN, 0)
        finish(DOWN, 0)
        keep(DOWN).wait()
        start_first(DOWN, 1)

    def stage3():
        for kind in (GATE, UP):
            rest(kind, 0)
            finish(kind, 0)
            keep(kind).wait()
            start_first(kind, 1)
            share(kind, 0).start()
        pass_on(DOWN, 1)

    def stage4():
        rest(DOWN, 1)
        finish(DOWN, 1)
        start_first(DOWN, 2)
        share(DOWN, 0).start()

    def stage5():
        for kind in (GATE, UP):
            pass_on(kind, 1)
        for kind in (GATE, UP):
            rest(kind, 1)
            share(kind, 1).start()
            share(kind, 2).start()

    def stage6():
        pass_on(DOWN, 2)
        rest(DOWN, 2)
        share(DOWN, 1).start()
        share(DOWN, 2).start()

    def stage7():
        for kind in (GATE, UP):
            finish(kind, 1)
            share(kind, 3).start()

    def stage8():
        finish(DOWN, 2)
        share(DOWN, 3).start()
        for kind in (GATE, UP, DOWN):
            for which in range(4):
                p = len(GATHER_ORDER[kind]) - 1
                ref = view(kind, p, SHARES[which], columns(SHARED, kind, 1 - core))
                arrived(ref, ds.at[kind, which], dr.at[kind, which])
        for kind in (GATE, UP):
            for by in (1, 3, 2):
                near(kind, by).wait_send()
        for kind in (GATE, UP, DOWN):
            for p in range(len(GATHER_ORDER[kind])):
                for n in range(2):
                    first(kind, p, n, 0).wait_send()
                    first(kind, p, n, 1).wait_send()
                    relay(kind, p, n).wait_send()
            for which in range(4):
                share(kind, which).wait_send()

    return [stage0, stage1, stage2, stage3, stage4, stage5, stage6, stage7, stage8]


def gather_scratch():
    dma = pltpu.SemaphoreType.DMA
    return [
        pltpu.VMEM((2, 3, D // 64, FF // 2), BF),
        pltpu.VMEM((2, D // 16, FF // 2), BF),
        dma((2, 3)),
        dma((2, 3)),
        dma((3, 3, 6)),
        dma((3, 3, 6)),
        dma((3, 4)),
        dma((3, 4)),
        dma((3,)),
    ]


VMEM, ANYWHERE = pl.BlockSpec(memory_space=pltpu.VMEM), pl.BlockSpec(memory_space=pl.ANY)


def gathered():
    wide = jax.ShapeDtypeStruct((4, 4, D // 16, FF), BF)
    return wide, wide, jax.ShapeDtypeStruct((4, 4, 4, FF // 64, D), BF)


def matrices(gate, up, down):
    return gate.reshape(D, FF), up.reshape(D, FF), down.reshape(FF, D)


SCATTER_ORDER = {GATE: (X, Y, Z), UP: (Y, X, Z), DOWN: (Z, X, Y)}
SPLIT = {GATE: 1280, UP: 1280, DOWN: 512}
COLS = {GATE: FF, UP: FF, DOWN: D}
BLOCKS = {
    GATE: ((4, 56), (1, 56), (1, 16)),
    UP: ((4, 56), (1, 56), (1, 16)),
    DOWN: ((16, 40), (4, 40), (1, 40)),
}
KINDS = (DOWN, GATE, UP)


def sums_of(phases):
    return (1,) if phases == (0,) else (1, 2)


def scatter_plan(phases, terms, outs, refs, carried=()):
    refs = list(refs)
    buf = {(k, p): [refs.pop(0) for _ in range(4)] for k in range(3) for p in phases}
    sums = sums_of(phases)
    wide = {(k, p): refs.pop(0) for k in range(3) for p in sums}
    stage = {(k, p): refs.pop(0) for k in range(3) for p in sums}
    own = {k: [refs.pop(0) for _ in range(3)] for k in range(3) if 0 in phases}
    ss, rs, ls, cs = refs
    core, at = place()

    def block(k, p, by):
        v = (at[SCATTER_ORDER[k][p]] + by) % 4
        if p:
            return stage[k, p].at[v]
        return terms[k].at[v] if k == GATE else terms[k].at[:, v]

    def part(k, n):
        return pl.ds(0, SPLIT[k]) if n == 0 else pl.ds(SPLIT[k], COLS[k] - SPLIT[k])

    def flow(k, p, n):
        from_left, from_right, left, right = buf[k, p]
        src, dst = {
            0: lambda: (block(k, p, 2).at[:, :, part(k, 0)], from_left),
            1: lambda: (block(k, p, 2).at[:, :, part(k, 1)], from_right),
            2: lambda: (block(k, p, 1).at[:, :, part(k, 1)], left.at[:, :, part(k, 1)]),
            3: lambda: (block(k, p, -1).at[:, :, part(k, 0)], right.at[:, :, part(k, 0)]),
            4: lambda: (from_left, left.at[:, :, part(k, 0)]),
            5: lambda: (from_right, right.at[:, :, part(k, 1)]),
        }[n]()
        to = moved(core, at, SCATTER_ORDER[k][p], (1, -1)[n % 2])
        sems = ss.at[k, p, n], rs.at[k, p, n]
        return pltpu.make_async_remote_copy(src, dst, *sems, device_id=to, device_id_type=MESH)

    def load(k, n):
        src = (lambda: block(k, 0, 1).at[:, :, part(k, 0)], lambda: block(k, 0, -1).at[:, :, part(k, 1)], lambda: block(k, 0, 0))[n]()
        return pltpu.make_async_copy(src, own[k][n], ls.at[k, n])

    def each(k, p, width, body):
        step = width if k == DOWN else 640
        count = width // step

        def one(i, carry):
            body(i // count, (i % count) * step, step)
            return carry

        lax.fori_loop(0, BLOCKS[k][p][0] * count, one, 0)

    def here(start, step):
        return pl.ds(pl.multiple_of(start, 128), step)

    def begin(k, p):
        for n in range(4):
            flow(k, p, n).start()
        if p == 0:
            for n in range(3):
                load(k, n).start()

    def middle(k, p):
        for n in range(2):
            flow(k, p, n).wait_recv()
            if p == 0:
                load(k, n).wait()
            come, before = buf[k, p][n], 0 if p == 0 or n == 0 else SPLIT[k]
            mine = own[k][n] if p == 0 else wide[k, p].at[(at[SCATTER_ORDER[k][p]] + (1, -1)[n]) % 4]

            def add(i, start, step, mine=mine, come=come, before=before):
                cols = here(start, step)
                come[i, :, cols] = (mine[i, :, here(start + before, step)].astype(F32) + come[i, :, cols].astype(F32)).astype(BF)

            each(k, p, SPLIT[k] if n == 0 else COLS[k] - SPLIT[k], add)
            flow(k, p, 4 + n).start()

    def end(k, p):
        left, right = buf[k, p][2:]
        for n in range(2, 6):
            flow(k, p, n).wait_recv()
        if p == 0:
            load(k, 2).wait()
        mine = own[k][2] if p == 0 else wide[k, p].at[at[SCATTER_ORDER[k][p]]]

        def add(i, start, step):
            cols = here(start, step)
            total = mine[i, :, cols].astype(F32) + left[i, :, cols].astype(F32) + right[i, :, cols].astype(F32)
            if p == 2:
                outs[k][:, cols] = total[: 40 if k == DOWN else 14].astype(BF)
            elif k != DOWN and p == 1:
                for z in range(4):
                    rows = jnp.concatenate([total[14 * z : 14 * z + 14], jnp.zeros((2, step), F32)], axis=0)
                    wide[k, 2][z, 0, :, cols] = rows
                    stage[k, 2][z, 0, :, cols] = rows.astype(BF)
            else:
                at_row = (i, 0) if k != DOWN or p == 1 else (i // 4, i % 4)
                wide[k, p + 1][(*at_row, slice(None), cols)] = total
                stage[k, p + 1][(*at_row, slice(None), cols)] = total.astype(BF)

        each(k, p, COLS[k], add)
        if p + 1 in phases:
            begin(k, p + 1)
        elif p == 0:
            for n in range(2):
                carry(k, n).start()

    def carry(k, n):
        here, there = (wide, stage)[n][k, 1], carried[3 * n + k]
        if 0 in phases:
            return pltpu.make_async_copy(here, there, cs.at[k, n])
        return pltpu.make_async_copy(there, here, cs.at[k, n])

    def enter():
        meet([moved(core, at, d, by) for d in (X, Y, Z) for by in (1, -1)])
        for k in KINDS:
            if 0 in phases:
                begin(k, 0)
            else:
                for n in range(2):
                    carry(k, 1 - n).start()

    def go_on():
        for k in KINDS:
            carry(k, 1).wait()
            begin(k, 1)
        for k in KINDS:
            carry(k, 0).wait()

    def leave():
        for k in KINDS:
            for p in phases:
                for n in range(6):
                    flow(k, p, n).wait_send()
            if phases == (0,):
                for n in range(2):
                    carry(k, n).wait()

    stages = [enter] if 0 in phases else [enter, go_on]
    for p in phases:
        stages += [functools.partial(middle, k, p) for k in KINDS]
        stages += [functools.partial(end, k, p) for k in KINDS]
    return [*stages, leave]


def scatter_scratch(phases):
    scratch = []
    for k in range(3):
        for p in phases:
            lead, rows = BLOCKS[k][p]
            for cols in (SPLIT[k], COLS[k] - SPLIT[k], COLS[k], COLS[k]):
                scratch.append(pltpu.VMEM((lead, rows, cols), BF))
    for kind in (F32, BF):
        for k in range(3):
            for p in sums_of(phases):
                lead, rows = BLOCKS[k][p]
                scratch.append(pltpu.VMEM((4, lead, rows, COLS[k]), kind))
    if 0 in phases:
        for k in range(3):
            lead, rows = BLOCKS[k][0]
            for cols in (SPLIT[k], COLS[k] - SPLIT[k], COLS[k]):
                scratch.append(pltpu.VMEM((lead, rows, cols), BF))
    dma = pltpu.SemaphoreType.DMA
    return [*scratch, dma((3, 3, 6)), dma((3, 3, 6)), dma((3, 3)), dma((3, 2))]


def carried_shapes():
    blocks = [(4, *BLOCKS[k][1], COLS[k]) for k in range(3)]
    return tuple(jax.ShapeDtypeStruct(shape, kind) for kind in (F32, BF) for shape in blocks)


def scattered():
    wide = jax.ShapeDtypeStruct((D // 64, FF), BF)
    return wide, wide, jax.ShapeDtypeStruct((FF // 64, D), BF)


def blocked(t_gate, t_up, t_down):
    return t_gate.reshape(4, 4, 56, FF), t_up.reshape(4, 4, 56, FF), t_down.reshape(16, 4, 40, D)


TOKENS, CHUNK = 2048, 512
GATHER_AT = ((2, 0), (3, 0), (5, 0), (7, 0))
FIRST_PHASE_AT = ((0, 0), *((2, 3), (3, 0), (3, 0)), *((7, 3), (7, 5), (7, 5)), (7, 5))
OTHER_PHASES_AT = ((0, 0), (0, 1), *[(1, 1)] * 3, *((2, 2), (3, 0), (3, 0)), *[(4, 0)] * 3, *[(4, 3)] * 3, (4, 3))
ALL_PHASES_AT = ((0, 0), *((3, 0), (3, 1), (4, 0)), *[(7, 2)] * 16)


def run(stages, places, number):
    for stage, (tile, chunk) in zip(stages, places, strict=True):
        if chunk == number:
            pl.when(pl.program_id(0) == tile)(stage)

ROWS = ((1,), (1,))
FIRST = ((0,), (0,))


def dot(a, b, over=((1,), (0,))):
    return lax.dot_general(a, b, (over, ((), ())), preferred_element_type=F32)


def norm(h):
    wide = h.astype(F32)
    scale = lax.rsqrt(jnp.mean(wide * wide, -1, keepdims=True) + 1e-6)
    return (wide * scale).astype(BF), scale


def chunks():
    return [slice(j, j + CHUNK) for j in range(0, FF, CHUNK)]


def forward_kernel(h_ref, *refs):
    given, refs = refs[:3], refs[3:]
    out_ref, first, second = refs[0], refs[1:4], refs[4:7]
    refs = refs[7:]
    count = len(gather_scratch())
    weights, sems = refs[2 * count : -1], refs[-1]
    now = gather_plan(0, given, first, refs[:count])
    later = gather_plan(1, given, second, refs[count : 2 * count], meeting=False)

    def bring(k, i):
        if k == DOWN:
            src, rows = first[k].at[i // 16, (i // 4) % 4, i % 4], FF // 64
        else:
            src, rows = first[k].at[i // 4, i % 4], D // 16
        return pltpu.make_async_copy(src, weights[k].at[pl.ds(pl.multiple_of(rows * i, 8), rows)], sems.at[k, i])

    def every(k, act):
        def one(i, carry):
            act(bring(k, i))
            return carry

        lax.fori_loop(0, 64 if k == DOWN else 16, one, 0)

    @pl.when(pl.program_id(0) == 0)
    def _():
        for stage in (*now[:2], later[0], now[2], later[1], now[3], later[2], *now[4:6], later[3], now[6], later[4], *now[7:]):
            stage()
        for k in range(3):
            every(k, lambda copy: copy.start())
        for k in range(3):
            every(k, lambda copy: copy.wait())

    gate_ref, up_ref, down_ref = weights
    h = h_ref[...]
    a, _ = norm(h)
    total = None
    for number, cols in enumerate(chunks()):
        run(later[5:], GATHER_AT, number)
        gate, up = dot(a, gate_ref[:, cols]), dot(a, up_ref[:, cols])
        act = (gate * jax.nn.sigmoid(gate) * up).astype(BF)
        more = dot(act, down_ref[cols, :])
        total = more if total is None else total + more
    out_ref[...] = h + total.astype(BF)


def hidden(a, by, cols, gate_ref, up_ref, down_ref, act_ref, by_gate_ref, by_up_ref):
    gate, up = dot(a, gate_ref[:, cols]), dot(a, up_ref[:, cols])
    by_act = dot(by, down_ref[cols, :], ROWS).astype(BF).astype(F32)
    sig = jax.nn.sigmoid(gate)
    silu = gate * sig
    act_ref[:, cols] = (silu * up).astype(BF)
    by_up = (by_act * silu).astype(BF)
    by_gate = (by_act * up * (sig + silu * (1 - sig))).astype(BF)
    by_up_ref[:, cols] = by_up
    by_gate_ref[:, cols] = by_gate


def norm_back(h, scale, by, by_a):
    by_a, wide = by_a.astype(BF).astype(F32), h.astype(F32)
    inner = jnp.mean(by_a * wide, -1, keepdims=True)
    return by + (by_a * scale - wide * (scale * scale * scale * inner)).astype(BF)


def backward_kernel(h_ref, by_ref, gate_ref, up_ref, down_ref, by_h_ref, a_ref, act_ref, by_gate_ref, by_up_ref):
    h, by = h_ref[...], by_ref[...]
    a, scale = norm(h)
    a_ref[...] = a
    for cols in chunks():
        hidden(a, by, cols, gate_ref, up_ref, down_ref, act_ref, by_gate_ref, by_up_ref)
    total = dot(by_gate_ref[...], gate_ref[...], ROWS) + dot(by_up_ref[...], up_ref[...], ROWS)
    by_h_ref[...] = norm_back(h, scale, by, total)


def inner_kernel(h_ref, by_ref, gate_ref, up_ref, down_ref, *refs):
    terms, (a_ref, act_ref, by_gate_ref, by_up_ref), carried = refs[:3], refs[3:7], refs[7:13]
    plan = scatter_plan((0,), terms, None, refs[13:], carried)
    a, _ = norm(h_ref[...])
    by = by_ref[...]
    a_ref[...] = a
    for number, cols in enumerate(chunks()):
        run(plan, FIRST_PHASE_AT, number)
        hidden(a, by, cols, gate_ref, up_ref, down_ref, act_ref, by_gate_ref, by_up_ref)
    run(plan, FIRST_PHASE_AT, len(chunks()))


def outer_kernel(h_ref, by_ref, by_gate_ref, by_up_ref, gate_ref, up_ref, *refs):
    terms, ready, out_ref, outs, refs = refs[:3], refs[3:6], refs[6], refs[7:10], refs[10:]
    plan = scatter_plan((0, 1, 2), terms, [out.at[0] for out in outs], refs)

    @pl.when(pl.program_id(0) == 0)
    def _():
        for k in range(3):
            outs[k][1] = ready[k][...]

    run(plan, ALL_PHASES_AT, 0)
    h = h_ref[...]
    _, scale = norm(h)
    total = dot(by_gate_ref[...], gate_ref[...], ROWS)
    run(plan, ALL_PHASES_AT, 1)
    total = total + dot(by_up_ref[...], up_ref[...], ROWS)
    out_ref[...] = norm_back(h, scale, by_ref[...], total)
    run(plan, ALL_PHASES_AT, 2)


def weights_kernel(hosts, a_ref, by_ref, act_ref, by_gate_ref, by_up_ref, *refs):
    plan, places = (), ()
    if hosts:
        plan, places = scatter_plan((1, 2), None, refs[9:12], refs[13:], refs[:6]), OTHER_PHASES_AT
        refs = refs[6:]
    t_gate_ref, t_up_ref, t_down_ref = refs[:3]
    turned = refs[6] if hosts else refs[3]

    @pl.when(pl.program_id(0) == 0)
    def _():
        turned[...] = a_ref[...].T

    run(plan, places, 0)
    t_down_ref[...] = dot(act_ref[...], by_ref[...], FIRST).astype(BF)
    run(plan, places, 1)
    t_gate_ref[...] = dot(turned[...], by_gate_ref[...]).astype(BF)
    run(plan, places, 2)
    t_up_ref[...] = dot(turned[...], by_up_ref[...]).astype(BF)
    run(plan, places, 3)


def whole(shape):
    return pl.BlockSpec(shape, lambda i: (0, 0), pipeline_mode=pl.Buffered(1))


def of_tokens(tile, cols):
    return pl.BlockSpec((tile, cols), lambda i: (i, 0))


def cost(matmuls):
    return pl.CostEstimate(flops=matmuls * 2 * TOKENS * D * FF, transcendentals=0, bytes_accessed=40_000_000)


def shaped(*shape):
    return jax.ShapeDtypeStruct(shape, BF)


def params(number=None):
    if number is None:
        return pltpu.CompilerParams(vmem_limit_bytes=BYTES)
    return pltpu.CompilerParams(collective_id=number, has_side_effects=True, vmem_limit_bytes=BYTES)


WEIGHTS = [whole((D, FF)), whole((D, FF)), whole((FF, D))]


def forward(h, shards):
    tile = TOKENS // 8
    h, *others = pl.pallas_call(
        forward_kernel,
        name="forward",
        grid=(TOKENS // tile,),
        out_shape=(shaped(TOKENS, D), *gathered(), *gathered()),
        in_specs=[of_tokens(tile, D), *[VMEM] * 3],
        out_specs=(of_tokens(tile, D), *[ANYWHERE] * 6),
        scratch_shapes=[
            *gather_scratch(),
            *gather_scratch(),
            pltpu.VMEM((D, FF), BF),
            pltpu.VMEM((D, FF), BF),
            pltpu.VMEM((FF, D), BF),
            pltpu.SemaphoreType.DMA((3, 64)),
        ],
        compiler_params=params(2),
        cost_estimate=cost(3),
    )(h, *shards)
    return h, matrices(*others[:3]), matrices(*others[3:])


def backward(h, by, weights):
    tile = TOKENS // 4
    return pl.pallas_call(
        backward_kernel,
        name="backward",
        grid=(TOKENS // tile,),
        out_shape=(shaped(TOKENS, D), shaped(TOKENS, D), *[shaped(TOKENS, FF)] * 3),
        in_specs=[of_tokens(tile, D), of_tokens(tile, D), *WEIGHTS],
        out_specs=(*[of_tokens(tile, D)] * 2, *[of_tokens(tile, FF)] * 3),
        compiler_params=params(),
        cost_estimate=cost(5),
    )(h, by, *weights)


def inner(h, by, weights, terms):
    tile = TOKENS // 8
    a, act, by_gate, by_up, *carried = pl.pallas_call(
        inner_kernel,
        name="inner",
        grid=(TOKENS // tile,),
        out_shape=(shaped(TOKENS, D), *[shaped(TOKENS, FF)] * 3, *carried_shapes()),
        in_specs=[of_tokens(tile, D), of_tokens(tile, D), *WEIGHTS, *[ANYWHERE] * 3],
        out_specs=(of_tokens(tile, D), *[of_tokens(tile, FF)] * 3, *[ANYWHERE] * 6),
        scratch_shapes=scatter_scratch((0,)),
        compiler_params=params(3),
        cost_estimate=cost(3),
    )(h, by, *weights, *blocked(*terms))
    return a, act, by_gate, by_up, carried


def outer(h, by, by_gate, by_up, weights, terms, ready):
    tile = TOKENS // 8
    by_h, *sums = pl.pallas_call(
        outer_kernel,
        name="outer",
        grid=(TOKENS // tile,),
        out_shape=(shaped(TOKENS, D), *(shaped(2, *like.shape) for like in scattered())),
        in_specs=[*[of_tokens(tile, D)] * 2, *[of_tokens(tile, FF)] * 2, *WEIGHTS[:2], *[ANYWHERE] * 3, *[VMEM] * 3],
        out_specs=(of_tokens(tile, D), *[VMEM] * 3),
        scratch_shapes=scatter_scratch((0, 1, 2)),
        compiler_params=params(4),
        cost_estimate=cost(2),
    )(h, by, by_gate, by_up, *weights[:2], *blocked(*terms), *ready)
    return by_h, sums


def weights_terms(a, by, act, by_gate, by_up, carried=()):
    side = pl.BlockSpec((TOKENS, CHUNK), lambda i: (0, i))
    hosts = bool(carried)
    t_gate, t_up, t_down, *sums = pl.pallas_call(
        functools.partial(weights_kernel, hosts),
        name="weights_sums" if hosts else "weights",
        grid=(FF // CHUNK,),
        out_shape=(shaped(D, FF), shaped(D, FF), shaped(FF, D), *(scattered() if hosts else ())),
        in_specs=[whole((TOKENS, D)), whole((TOKENS, D)), side, side, side, *[ANYWHERE] * len(carried)],
        out_specs=(
            pl.BlockSpec((D, CHUNK), lambda i: (0, i)),
            pl.BlockSpec((D, CHUNK), lambda i: (0, i)),
            pl.BlockSpec((CHUNK, D), lambda i: (i, 0)),
            *([VMEM] * 3 if hosts else ()),
        ),
        scratch_shapes=[pltpu.VMEM((D, TOKENS), BF), *(scatter_scratch((1, 2)) if hosts else ())],
        compiler_params=params(5 if hosts else None),
        cost_estimate=cost(3),
    )(a, by, act, by_gate, by_up, *carried)
    return (t_gate, t_up, t_down), sums


def local(x, dy, *shards):
    x, dy = x[0], dy[0]
    h, first, second = forward(x, shards)
    by_h, *saved = backward(h, dy, second)
    a, act, by_gate, by_up = saved
    terms, _ = weights_terms(a, dy, act, by_gate, by_up)
    a, act, by_gate, by_up, carried = inner(x, by_h, first, terms)
    terms, of_second = weights_terms(a, by_h, act, by_gate, by_up, carried)
    by_x, sums = outer(x, by_h, by_gate, by_up, first, terms, of_second)
    return (by_x[None], *sums)


def solution(mesh):
    tokens, rows = P(("rep", "dp")), P(None, "dp", None)
    return jax.shard_map(
        local,
        mesh=mesh,
        in_specs=(tokens, tokens, rows, rows, rows),
        out_specs=(tokens, *([P("rep", "dp", None)] * 3)),
        check_vma=False,
    )
```

time: 464 us -> 427 us (0.920); the launches traced: 463 us -> 421 us
  Pallas kernels: 450 us -> 409 us
    pallas_call x6 -> x5, Pallas kernels: 375 us -> 287 us  [the longest x2 90.4 us: weights_terms(): pl.pallas_call(functools.partial(weights_kernel, hosts), name='weights_su...]
    pallas_call x1, Pallas kernels: 75.1 us -> 121 us  [forward(): pl.pallas_call(forward_kernel, name='forward', grid=(TOKENS // tile,), ou...]
    unnamed x11 -> x8, local copies, waits for them, and re-layouts: 8.97 us -> 11.5 us
where the time goes in v3:
time: 427 us; the launch traced here: 421 us
  Pallas kernels  409 us (96%)
  local copies, waits for them, and re-layouts  11.5 us (3%)
    pallas_call x1, Pallas kernels, forward(): pl.pallas_call(forward_kernel, name='forward', grid=(TOKENS // tile,), ou...  121 us
    pallas_call x2, Pallas kernels, weights_terms(): pl.pallas_call(functools.partial(weights_kernel, hosts), name='weights_su...  90.4 us
    pallas_call x1, Pallas kernels, backward(): pl.pallas_call(backward_kernel, name='backward', grid=(TOKENS // tile,),...  68.4 us
    pallas_call x1, Pallas kernels, outer(): pl.pallas_call(outer_kernel, name='outer', grid=(TOKENS // tile,), out_sh...  68 us
    pallas_call x1, Pallas kernels, inner(): pl.pallas_call(inner_kernel, name='inner', grid=(TOKENS // tile,), out_sh...  60.5 us
    unnamed x8, local copies, waits for them, and re-layouts  11.5 us

profile of v3, /device:TPU:0, one launch (start us, length us, event | category | flops | bytes accessed | tf_op | source)
XLA Modules:
  0.0 421.3 jit_solution(8554921549439829336)
XLA Ops:
  0.6 1.6 copy.9.refs_0_
  2.2 1.6 copy.10.refs_1_
  3.8 121.3 %forward.1 = (bf16[2048,896]{1,0:T(8,128)(2,1)}, bf16[4,4,56,2560]{3,2,1,0:T(8,128)(2,1)}, bf16[4,4,56,2560]{3,2,1,0:T(8,128)(2,1)}, bf16[4,4,4,40,896]{4,3,2,1,...) custom-call(bf16[2048,896]{1,0:T(8,128)(2,1)} %bitcast.18, ...), custom_call_target="tpu_custom_call" | custom-call | flops 28185722880 | bytes 40000000 | tf_op jit(solution)/shard_map/forward/pallas_call | solution.py:615
  125.1 68.4 %backward.1 = (bf16[2048,896]{1,0:T(8,128)(2,1)}, bf16[2048,896]{1,0:T(8,128)(2,1)}, bf16[2048,2560]{1,0:T(8,128)(2,1)}, bf16[2048,2560]{1,0:T(8,128)(2,1)}, bf16[2048,2560]{1,0:T(8,128)(2,1)}) custom-call(bf16[2048,896]{1,0:T(8,128)(2,1)} %get-tuple-element.39.h_ref, bf16[2048,896]{1,0:T(8,128)(2,1)} %bitcast.16, bf16[896,2560]{1,0:T(8,128)(2,1)} %bitcast.32, ...), custom_call_target="tpu_custom_call" | custom-call | flops 46976204800 | bytes 40000000 | tf_op jit(solution)/shard_map/backward/pallas_call | solution.py:638
  193.6 39.1 %weights.1 = (bf16[896,2560]{1,0:T(8,128)(2,1)}, bf16[896,2560]{1,0:T(8,128)(2,1)}, bf16[2560,896]{1,0:T(8,128)(2,1)}) custom-call(bf16[2048,896]{1,0:T(8,128)(2,1)} %get-tuple-element.47.a_ref, bf16[2048,896]{1,0:T(8,128)(2,1)} %bitcast.17, bf16[2048,2560]{1,0:T(8,128)(2,1)} %get-tuple-element.48.act_ref, bf16[2048,2560]{1,0:T(8,128)(2,1)} %get-tuple-element.49.by_gate_ref, ...), custom_call_target="tpu_custom_call" | custom-call | flops 28185722880 | bytes 40000000 | tf_op jit(solution)/shard_map/weights/pallas_call | solution.py:685
  232.7 60.5 %inner.1 = (bf16[2048,896]{1,0:T(8,128)(2,1)}, bf16[2048,2560]{1,0:T(8,128)(2,1)}, bf16[2048,2560]{1,0:T(8,128)(2,1)}, bf16[2048,2560]{1,0:T(8,128)(2,1)}, f32[4...) custom-call(bf16[2048,896]{1,0:T(8,128)(2,1)} %bitcast.19, ...), custom_call_target="tpu_custom_call" | custom-call | flops 28185722880 | bytes 40000000 | tf_op jit(solution)/shard_map/inner/pallas_call | solution.py:652
  293.2 51.3 %weights_sums.1 = (bf16[896,2560]{1,0:T(8,128)(2,1)}, bf16[896,2560]{1,0:T(8,128)(2,1)}, bf16[2560,896]{1,0:T(8,128)(2,1)}, bf16[14,2560]{1,0:T(8,128)(2,1)}, bf...) custom-call(bf16[2048,896]{1,0:T(8,128)(2,1)} %get-tuple-element.56.a_ref, bf16[2048,896]{1,0:T(8,128)(2,1)} %get-tuple-element.43.by_ref, ...), custom_call_target="tpu_custom_call" | custom-call | flops 28185722880 | bytes 40000000 | tf_op jit(solution)/shard_map/weights_sums/pallas_call | solution.py:685
  344.5 68.0 %outer.1 = (bf16[2048,896]{1,0:T(8,128)(2,1)}, bf16[2,14,2560]{2,1,0:T(8,128)(2,1)}, bf16[2,14,2560]{2,1,0:T(8,128)(2,1)}, bf16[2,40,896]{2,1,0:T(8,128)(2,1)}) custom-call(bf16[2048,896]{1,0:T(8,128)(2,1)} %bitcast.20, bf16[2048,896]{1,0:T(8,128)(2,1)} %get-tuple-element.43.by_ref, bf16[2048,2560]{1,0:T(8,128)(2,1)} %get-tuple-element.54.by_gate_ref, ...), custom_call_target="tpu_custom_call" | custom-call | flops 18790481920 | bytes 40000000 | tf_op jit(solution)/shard_map/outer/pallas_call | solution.py:668
  412.5 0.0 copy-start
  412.5 1.8 copy.11
  414.3 1.7 copy.12
  416.0 4.2 copy.15
  420.2 0.0 copy-done
  420.2 0.7 copy.16
Async XLA Ops:
  412.5 7.7 %copy-start = (bf16[2,40,896]{2,1,0:T(8,128)(2,1)S(1)}, bf16[2,40,896]{2,1,0:T(8,128)(2,1)}, u32[]{:S(2)}) copy-start(bf16[2,40,896]{2,1,0:T(8,128)(2,1)} %get-tuple-element.85) | copy-start | bytes 430084

commit v4 on v3

--- a/solution.py
+++ b/solution.py
@@ -432,7 +432,7 @@
 
 TOKENS, CHUNK = 2048, 512
 GATHER_AT = ((2, 0), (3, 0), (5, 0), (7, 0))
-FIRST_PHASE_AT = ((0, 0), *((2, 3), (3, 0), (3, 0)), *((7, 3), (7, 5), (7, 5)), (7, 5))
+FIRST_PHASE_AT = ((0, 0), *((4, 0), (4, 3), (4, 3)), *((7, 5), (7, 5), (7, 5)), (7, 5))
 OTHER_PHASES_AT = ((0, 0), (0, 1), *[(1, 1)] * 3, *((2, 2), (3, 0), (3, 0)), *[(4, 0)] * 3, *[(4, 3)] * 3, (4, 3))
 ALL_PHASES_AT = ((0, 0), *((3, 0), (3, 1), (4, 0)), *[(7, 2)] * 16)
 
@@ -462,8 +462,8 @@
 
 def forward_kernel(h_ref, *refs):
     given, refs = refs[:3], refs[3:]
-    out_ref, first, second = refs[0], refs[1:4], refs[4:7]
-    refs = refs[7:]
+    out_ref, a_ref, keep_gate_ref, keep_up_ref, first, second = *refs[:4], refs[4:7], refs[7:10]
+    refs = refs[10:]
     count = len(gather_scratch())
     weights, sems = refs[2 * count : -1], refs[-1]
     now = gather_plan(0, given, first, refs[:count])
@@ -495,18 +495,20 @@
     gate_ref, up_ref, down_ref = weights
     h = h_ref[...]
     a, _ = norm(h)
+    a_ref[...] = a
     total = None
     for number, cols in enumerate(chunks()):
         run(later[5:], GATHER_AT, number)
         gate, up = dot(a, gate_ref[:, cols]), dot(a, up_ref[:, cols])
+        keep_gate_ref[:, cols] = gate
+        keep_up_ref[:, cols] = up
         act = (gate * jax.nn.sigmoid(gate) * up).astype(BF)
         more = dot(act, down_ref[cols, :])
         total = more if total is None else total + more
     out_ref[...] = h + total.astype(BF)
 
 
-def hidden(a, by, cols, gate_ref, up_ref, down_ref, act_ref, by_gate_ref, by_up_ref):
-    gate, up = dot(a, gate_ref[:, cols]), dot(a, up_ref[:, cols])
+def hidden(gate, up, by, cols, down_ref, act_ref, by_gate_ref, by_up_ref):
     by_act = dot(by, down_ref[cols, :], ROWS).astype(BF).astype(F32)
     sig = jax.nn.sigmoid(gate)
     silu = gate * sig
@@ -528,20 +530,19 @@
     a, scale = norm(h)
     a_ref[...] = a
     for cols in chunks():
-        hidden(a, by, cols, gate_ref, up_ref, down_ref, act_ref, by_gate_ref, by_up_ref)
+        gate, up = dot(a, gate_ref[:, cols]), dot(a, up_ref[:, cols])
+        hidden(gate, up, by, cols, down_ref, act_ref, by_gate_ref, by_up_ref)
     total = dot(by_gate_ref[...], gate_ref[...], ROWS) + dot(by_up_ref[...], up_ref[...], ROWS)
     by_h_ref[...] = norm_back(h, scale, by, total)
 
 
-def inner_kernel(h_ref, by_ref, gate_ref, up_ref, down_ref, *refs):
-    terms, (a_ref, act_ref, by_gate_ref, by_up_ref), carried = refs[:3], refs[3:7], refs[7:13]
-    plan = scatter_plan((0,), terms, None, refs[13:], carried)
-    a, _ = norm(h_ref[...])
+def inner_kernel(by_ref, gate_ref, up_ref, down_ref, *refs):
+    terms, results, carried = refs[:3], refs[3:6], refs[6:12]
+    plan = scatter_plan((0,), terms, None, refs[12:], carried)
     by = by_ref[...]
-    a_ref[...] = a
     for number, cols in enumerate(chunks()):
         run(plan, FIRST_PHASE_AT, number)
-        hidden(a, by, cols, gate_ref, up_ref, down_ref, act_ref, by_gate_ref, by_up_ref)
+        hidden(gate_ref[:, cols], up_ref[:, cols], by, cols, down_ref, *results)
     run(plan, FIRST_PHASE_AT, len(chunks()))
 
 
@@ -612,13 +613,13 @@
 
 def forward(h, shards):
     tile = TOKENS // 8
-    h, *others = pl.pallas_call(
+    h, a, gate, up, *others = pl.pallas_call(
         forward_kernel,
         name="forward",
         grid=(TOKENS // tile,),
-        out_shape=(shaped(TOKENS, D), *gathered(), *gathered()),
+        out_shape=(*[shaped(TOKENS, D)] * 2, *[jax.ShapeDtypeStruct((TOKENS, FF), F32)] * 2, *gathered(), *gathered()),
         in_specs=[of_tokens(tile, D), *[VMEM] * 3],
-        out_specs=(of_tokens(tile, D), *[ANYWHERE] * 6),
+        out_specs=(*[of_tokens(tile, D)] * 2, *[of_tokens(tile, FF)] * 2, *[ANYWHERE] * 6),
         scratch_shapes=[
             *gather_scratch(),
             *gather_scratch(),
@@ -630,7 +631,7 @@
         compiler_params=params(2),
         cost_estimate=cost(3),
     )(h, *shards)
-    return h, matrices(*others[:3]), matrices(*others[3:])
+    return h, (a, gate, up), matrices(*others[:3]), matrices(*others[3:])
 
 
 def backward(h, by, weights):
@@ -647,20 +648,20 @@
     )(h, by, *weights)
 
 
-def inner(h, by, weights, terms):
+def inner(by, gate, up, w_down, terms):
     tile = TOKENS // 8
-    a, act, by_gate, by_up, *carried = pl.pallas_call(
+    act, by_gate, by_up, *carried = pl.pallas_call(
         inner_kernel,
         name="inner",
         grid=(TOKENS // tile,),
-        out_shape=(shaped(TOKENS, D), *[shaped(TOKENS, FF)] * 3, *carried_shapes()),
-        in_specs=[of_tokens(tile, D), of_tokens(tile, D), *WEIGHTS, *[ANYWHERE] * 3],
-        out_specs=(of_tokens(tile, D), *[of_tokens(tile, FF)] * 3, *[ANYWHERE] * 6),
+        out_shape=(*[shaped(TOKENS, FF)] * 3, *carried_shapes()),
+        in_specs=[of_tokens(tile, D), *[of_tokens(tile, FF)] * 2, WEIGHTS[2], *[ANYWHERE] * 3],
+        out_specs=(*[of_tokens(tile, FF)] * 3, *[ANYWHERE] * 6),
         scratch_shapes=scatter_scratch((0,)),
         compiler_params=params(3),
-        cost_estimate=cost(3),
-    )(h, by, *weights, *blocked(*terms))
-    return a, act, by_gate, by_up, carried
+        cost_estimate=cost(1),
+    )(by, gate, up, w_down, *blocked(*terms))
+    return act, by_gate, by_up, carried
 
 
 def outer(h, by, by_gate, by_up, weights, terms, ready):
@@ -703,12 +704,12 @@
 
 def local(x, dy, *shards):
     x, dy = x[0], dy[0]
-    h, first, second = forward(x, shards)
+    h, (a0, gate, up), first, second = forward(x, shards)
     by_h, *saved = backward(h, dy, second)
     a, act, by_gate, by_up = saved
     terms, _ = weights_terms(a, dy, act, by_gate, by_up)
-    a, act, by_gate, by_up, carried = inner(x, by_h, first, terms)
-    terms, of_second = weights_terms(a, by_h, act, by_gate, by_up, carried)
+    act, by_gate, by_up, carried = inner(by_h, gate, up, first[2], terms)
+    terms, of_second = weights_terms(a0, by_h, act, by_gate, by_up, carried)
     by_x, sums = outer(x, by_h, by_gate, by_up, first, terms, of_second)
     return (by_x[None], *sums)
 

time: 427 us -> 419 us (0.981); the launches traced: 421 us -> 419 us
    pallas_call x1, Pallas kernels: 60.5 us -> 54.7 us  [inner(): pl.pallas_call(inner_kernel, name='inner', grid=(TOKENS // tile,), out_sh...]
where the time goes in v4:
time: 419 us
  Pallas kernels  407 us (97%)
  local copies, waits for them, and re-layouts  11.5 us (3%)
    pallas_call x1, Pallas kernels, forward(): pl.pallas_call(forward_kernel, name='forward', grid=(TOKENS // tile,), ou...  123 us
    pallas_call x2, Pallas kernels, weights_terms(): pl.pallas_call(functools.partial(weights_kernel, hosts), name='weights_su...  90.5 us
    pallas_call x1, Pallas kernels, outer(): pl.pallas_call(outer_kernel, name='outer', grid=(TOKENS // tile,), out_sh...  70.3 us
    pallas_call x1, Pallas kernels, backward(): pl.pallas_call(backward_kernel, name='backward', grid=(TOKENS // tile,),...  68.4 us
    pallas_call x1, Pallas kernels, inner(): pl.pallas_call(inner_kernel, name='inner', grid=(TOKENS // tile,), out_sh...  54.7 us
    unnamed x8, local copies, waits for them, and re-layouts  11.5 us

profile of v4, /device:TPU:0, one launch (start us, length us, event | category | flops | bytes accessed | tf_op | source)
XLA Modules:
  0.0 419.1 jit_solution(1689680747727329229)
XLA Ops:
  0.6 1.6 copy.9.refs_0_
  2.2 1.6 copy.10.refs_1_
  3.8 123.0 %forward.1 = (bf16[2048,896]{1,0:T(8,128)(2,1)}, bf16[2048,896]{1,0:T(8,128)(2,1)}, f32[2048,2560]{1,0:T(8,128)}, f32[2048,2560]{1,0:T(8,128)}, bf16[4,4,56,2560...) custom-call(bf16[2048,896]{1,0:T(8,128)(2,1)} %bitcast.22, ...), custom_call_target="tpu_custom_call" | custom-call | flops 28185722880 | bytes 40000000 | tf_op jit(solution)/shard_map/forward/pallas_call | solution.py:616
  126.8 68.4 %backward.1 = (bf16[2048,896]{1,0:T(8,128)(2,1)}, bf16[2048,896]{1,0:T(8,128)(2,1)}, bf16[2048,2560]{1,0:T(8,128)(2,1)}, bf16[2048,2560]{1,0:T(8,128)(2,1)}, bf16[2048,2560]{1,0:T(8,128)(2,1)}) custom-call(bf16[2048,896]{1,0:T(8,128)(2,1)} %get-tuple-element.41.h_ref, bf16[2048,896]{1,0:T(8,128)(2,1)} %bitcast.20, bf16[896,2560]{1,0:T(8,128)(2,1)} %bitcast.29, ...), custom_call_target="tpu_custom_call" | custom-call | flops 46976204800 | bytes 40000000 | tf_op jit(solution)/shard_map/backward/pallas_call | solution.py:639
  195.2 39.1 %weights.1 = (bf16[896,2560]{1,0:T(8,128)(2,1)}, bf16[896,2560]{1,0:T(8,128)(2,1)}, bf16[2560,896]{1,0:T(8,128)(2,1)}) custom-call(bf16[2048,896]{1,0:T(8,128)(2,1)} %get-tuple-element.49.a_ref, bf16[2048,896]{1,0:T(8,128)(2,1)} %bitcast.21, bf16[2048,2560]{1,0:T(8,128)(2,1)} %get-tuple-element.50.act_ref, bf16[2048,2560]{1,0:T(8,128)(2,1)} %get-tuple-element.51.by_gate_ref, ...), custom_call_target="tpu_custom_call" | custom-call | flops 28185722880 | bytes 40000000 | tf_op jit(solution)/shard_map/weights/pallas_call | solution.py:686
  234.3 54.7 %inner.1 = (bf16[2048,2560]{1,0:T(8,128)(2,1)}, bf16[2048,2560]{1,0:T(8,128)(2,1)}, bf16[2048,2560]{1,0:T(8,128)(2,1)}, f32[4,1,56,2560]{3,2,1,0:T(8,128)}, f32[...) custom-call(bf16[2048,896]{1,0:T(8,128)(2,1)} %get-tuple-element.45., ...), custom_call_target="tpu_custom_call" | custom-call | flops 9395240960 | bytes 40000000 | tf_op jit(solution)/shard_map/inner/pallas_call | solution.py:653
  289.0 51.4 %weights_sums.1 = (bf16[896,2560]{1,0:T(8,128)(2,1)}, bf16[896,2560]{1,0:T(8,128)(2,1)}, bf16[2560,896]{1,0:T(8,128)(2,1)}, bf16[14,2560]{1,0:T(8,128)(2,1)}, bf...) custom-call(bf16[2048,896]{1,0:T(8,128)(2,1)} %get-tuple-element.60.a_ref, bf16[2048,896]{1,0:T(8,128)(2,1)} %get-tuple-element.45.by_ref, ...), custom_call_target="tpu_custom_call" | custom-call | flops 28185722880 | bytes 40000000 | tf_op jit(solution)/shard_map/weights_sums/pallas_call | solution.py:686
  340.5 70.3 %outer.1 = (bf16[2048,896]{1,0:T(8,128)(2,1)}, bf16[2,14,2560]{2,1,0:T(8,128)(2,1)}, bf16[2,14,2560]{2,1,0:T(8,128)(2,1)}, bf16[2,40,896]{2,1,0:T(8,128)(2,1)}) custom-call(bf16[2048,896]{1,0:T(8,128)(2,1)} %bitcast.23, bf16[2048,896]{1,0:T(8,128)(2,1)} %get-tuple-element.45.by_ref, bf16[2048,2560]{1,0:T(8,128)(2,1)} %get-tuple-element.56.by_gate_ref, ...), custom_call_target="tpu_custom_call" | custom-call | flops 18790481920 | bytes 40000000 | tf_op jit(solution)/shard_map/outer/pallas_call | solution.py:669
  410.8 0.0 copy-start
  410.8 1.8 copy.11
  412.5 1.7 copy.12
  414.3 4.2 copy.15
  418.4 0.0 copy-done
  418.4 0.7 copy.16
Async XLA Ops:
  410.8 7.7 %copy-start = (bf16[2,40,896]{2,1,0:T(8,128)(2,1)S(1)}, bf16[2,40,896]{2,1,0:T(8,128)(2,1)}, u32[]{:S(2)}) copy-start(bf16[2,40,896]{2,1,0:T(8,128)(2,1)} %get-tuple-element.89) | copy-start | bytes 430084
